TPU v7x, 32 devices: a whole 2x2x4 slice. The times are simulated.
32 devices in a mesh: shard: 16 (over z, y, core), model: 2 (over x).
Axes of the slice: x: 2, y: 2, z: 4, core: 2. Of those that a mesh axis runs over, the one named last changes fastest.
Arguments:
- gradients: float32 [128, 128, 4096], P(None, 'shard', 'model'), may hold values from -6 to 6
- momentum: float32 [128, 128, 4096], P(None, 'shard', 'model'), may hold values from -6 to 6
- weights: float32 [128, 128, 4096], P(None, 'shard', 'model'), may hold values from -0.1875 to 0.1875
Outputs:
- new_weights: float32 [128, 128, 4096], P(None, 'shard', 'model')
- new_momentum: float32 [128, 128, 4096], P(None, 'shard', 'model')
All inputs are finite; a program needn't handle non-finite values.
Results may differ from a plain program's by a relative error of at most 0.0001.
Values sent between devices are 32-bit elements; how exact they have to be, the bound alone decides.
No kernel may reach another device: no remote copies, remote signals or barrier semaphores. Data moves between devices by JAX's collectives and lax.ppermute only.
A program may use at most 128 MiB of HBM per device.

v0:
```python
import functools

import jax
import jax.numpy as jnp
from jax import lax
from jax.experimental import pallas as pl
from jax.experimental.pallas import tpu as pltpu
from jax.sharding import PartitionSpec as P


ITERS = 3
CHUNKS = 2
FAR = 6
NEAR = 6
LATER = 1
HEAD = (2, 6)
TAIL = 3
LAST = (8, 4)

hold_rate = 0.9
learn_rate = 0.9
decay_rate = 0.1


def mm(form, a, b):
    return jnp.einsum(form, a, b, precision=lax.Precision.HIGHEST)


def dot(a, b, contract_b=0):
    return lax.dot_general(
        a, b, (((1,), (contract_b,)), ((), ())),
        precision=lax.Precision.HIGHEST, preferred_element_type=jnp.float32,
    )


def cost(flops, moved):
    return pl.CostEstimate(flops=flops, bytes_accessed=moved, transcendentals=0)


def around(part, axis):
    size = lax.axis_size(axis)
    return [lax.ppermute(part, axis, [(i, (i + hop) % size) for i in range(size)]) for hop in range(1, size)]


def polynomial(raw, product):
    side = raw.shape[-1]
    place = raw.shape[:-2] + (side, side)
    eye = (lax.broadcasted_iota(jnp.int32, place, raw.ndim - 2) == lax.broadcasted_iota(jnp.int32, place, raw.ndim - 1)).astype(jnp.float32)
    total = jnp.sum(jnp.sum(raw * eye, axis=-1, keepdims=True), axis=-2, keepdims=True)
    scale = lax.rsqrt(total + 1e-06)
    gram = (raw * scale) * scale
    chain = None
    for step in range(ITERS):
        poly = 3.4445 * eye - 4.775 * gram + 2.0315 * product(gram, gram)
        chain = poly if chain is None else product(poly, chain)
        if step < ITERS - 1:
            gram = product(poly, product(gram, poly))
    return chain * scale


def places(flips, held, rows, columns, chunk):
    def spot(i, me):
        flip = flips[0]
        for k in range(1, len(flips)):
            flip = jnp.where(i == k, flips[k], flip)
        return ((me[0] ^ flip) * CHUNKS + chunk, 0, 0)

    return pl.BlockSpec((held, rows, columns), spot)


def momentum_kernel(count, me_ref, gradients_ref, momentum_ref, *refs):
    whole_ref, piece_refs = refs[-count - 1], refs[-count:]
    fresh = hold_rate * momentum_ref[...] + gradients_ref[...]
    whole_ref[...] = fresh
    for k in range(count):
        @pl.when(pl.program_id(0) == k)
        def _():
            piece_refs[k][...] = fresh


def momentum_of(me, flips, chunk, held, gradients, momentum, whole):
    _, rows, columns = gradients.shape
    count = len(flips)
    there = places(flips, held, rows, columns, chunk)
    here = pl.BlockSpec((held, rows, columns), lambda i, me: (0, 0, 0))
    size = count * held * rows * columns
    more = [] if whole is None else [whole]
    return pl.pallas_call(
        functools.partial(momentum_kernel, count),
        grid_spec=pltpu.PrefetchScalarGridSpec(
            num_scalar_prefetch=1,
            grid=(count,),
            in_specs=[there, there] + [pl.BlockSpec(memory_space=pl.ANY)] * len(more),
            out_specs=[there] + [here] * count,
        ),
        out_shape=[jax.ShapeDtypeStruct(gradients.shape, jnp.float32)]
        + [jax.ShapeDtypeStruct((held, rows, columns), jnp.float32)] * count,
        input_output_aliases={3: 0} if more else {},
        cost_estimate=cost(2 * size, 16 * size),
        name="momentum",
    )(me, gradients, momentum, *more)


def weights_kernel(count, me_ref, weights_ref, *refs):
    for k in range(count):
        @pl.when(pl.program_id(0) == k)
        def _():
            refs[-1][...] = (1.0 - learn_rate * decay_rate) * weights_ref[...] - learn_rate * refs[k][...]


def weights_of(me, flips, chunk, weights, back, whole):
    _, rows, columns = weights.shape
    count, held = len(flips), back[0].shape[0]
    there = places(flips, held, rows, columns, chunk)
    here = pl.BlockSpec((held, rows, columns), lambda i, me: (0, 0, 0))
    size = count * held * rows * columns
    more = [] if whole is None else [whole]
    return pl.pallas_call(
        functools.partial(weights_kernel, count),
        grid_spec=pltpu.PrefetchScalarGridSpec(
            num_scalar_prefetch=1,
            grid=(count,),
            in_specs=[there] + [here] * count + [pl.BlockSpec(memory_space=pl.ANY)] * len(more),
            out_specs=there,
        ),
        out_shape=jax.ShapeDtypeStruct(weights.shape, jnp.float32),
        input_output_aliases={2 + count: 0} if more else {},
        cost_estimate=cost(3 * size, 12 * size),
        name="weights",
    )(me, weights, *back, *more)


def stacked(refs):
    return jnp.concatenate([ref[0] for ref in refs], axis=0)


def gram_kernel(*refs):
    stack = stacked(refs[:-1])
    refs[-1][0] = dot(stack, stack, 1)


def gram_of(pieces):
    held, rows, columns = pieces[0].shape
    side = len(pieces) * rows
    return pl.pallas_call(
        gram_kernel,
        grid=(held,),
        in_specs=[pl.BlockSpec((1, rows, columns), lambda i: (i, 0, 0))] * len(pieces),
        out_specs=pl.BlockSpec((1, side, side), lambda i: (i, 0, 0)),
        out_shape=jax.ShapeDtypeStruct((held, side, side), jnp.float32),
        cost_estimate=cost(12 * held * side * side * columns, 4 * held * side * columns),
        name="gram",
    )(*pieces)


def apply_kernel(parts, count, *refs):
    raw = refs[0][0]
    for ref in refs[1:parts]:
        raw = raw + ref[0]
    found = dot(polynomial(raw, dot), stacked(refs[parts:parts + count]))
    rows = found.shape[0] // count
    for k in range(count):
        refs[parts + count + k][0] = found[k * rows:(k + 1) * rows]


def apply_of(grams, pieces):
    held, rows, columns = pieces[0].shape
    side = len(pieces) * rows
    square = pl.BlockSpec((1, side, side), lambda i: (i, 0, 0))
    strip = pl.BlockSpec((1, rows, columns), lambda i: (i, 0, 0))
    return pl.pallas_call(
        functools.partial(apply_kernel, len(grams), len(pieces)),
        grid=(held,),
        in_specs=[square] * len(grams) + [strip] * len(pieces),
        out_specs=[strip] * len(pieces),
        out_shape=[jax.ShapeDtypeStruct((held, rows, columns), jnp.float32)] * len(pieces),
        cost_estimate=cost(12 * held * side * side * (columns + 9 * side), 8 * held * side * columns),
        name="apply",
    )(*grams, *pieces)


def woven(far, near):
    flips = []
    for k in range(max(len(far), len(near))):
        flips += far[k:k + 1] + near[k:k + 1]
    return flips


def cut(flips, sizes):
    runs = []
    for size in sizes:
        runs.append(tuple(flips[:size]))
        flips = flips[size:]
    return runs + [tuple(flips)] * bool(flips)


def plan(owners):
    half = owners // 2
    far, near = list(range(half, owners)), list(range(1, half))
    flips = woven(far, near)
    due = []
    for c in range(CHUNKS):
        place = half * (c + 1) + FAR
        due.append((min(place, half * (CHUNKS + c)), ("gram", c)))
        due.append((min(place + LATER, half * (CHUNKS + c)), ("apply", c)))
        if c:
            due.append((half * (c - 1) + FAR - 1, ("momentum", c, tuple(flips + [0]))))
        if c < CHUNKS - 1:
            due.append((half * (CHUNKS + c + 1) + FAR, ("weights", c, tuple([0] + flips))))
    due.sort(key=lambda one: one[0])
    steps, gone = [], 0
    heads = cut(flips + [0], HEAD)
    steps.append(("momentum", 0, heads[0]))
    rest, ready = heads[1:], set(heads[0])
    for kind in ("in", "out"):
        for c in range(CHUNKS):
            order = flips if (kind, c) != ("out", CHUNKS - 1) else woven(far[:-TAIL], near) + far[-TAIL:]
            for flip in order:
                while kind == "in" and c == 0 and flip not in ready:
                    steps.append(("momentum", 0, rest[0]))
                    ready |= set(rest.pop(0))
                while flip in far and due and due[0][0] <= gone:
                    steps.append(due.pop(0)[1])
                steps.append((kind, c, flip))
                gone += flip in far
    steps += [one for _, one in due]
    return steps + [("weights", CHUNKS - 1, run) for run in cut([0] + order, LAST)]


def body(gradients, momentum, weights):
    owners = lax.axis_size("shard")
    mats, _, _ = gradients.shape
    held = mats // (CHUNKS * owners)
    tick = lax.axis_index("shard").astype(jnp.int32)
    me = tick.reshape(1)
    whole, updated, ticks = None, None, 0
    pieces, arrived, grams, found, back = {}, {}, {}, {}, {}
    ends, gates = {True: [], False: []}, []

    def send(piece, flip):
        far = flip >= owners // 2
        window = FAR if far else NEAR
        before = gates + ends[far][-window:][:len(ends[far]) >= window]
        if before:
            piece = lax.optimization_barrier((piece, *before))[0]
        gates.clear()
        ends[far].append(lax.ppermute(piece, "shard", [(i, i ^ flip) for i in range(owners)]))
        return ends[far][-1]

    for kind, c, *more in plan(owners):
        if kind == "momentum":
            whole, *some = momentum_of(me, more[0], c, held, gradients, momentum, whole)
            pieces.update(zip([(c, flip) for flip in more[0]], some))
            gates.append(whole)
        elif kind == "in":
            arrived[c, more[0]] = send(pieces[c, more[0]], more[0])
        elif kind == "gram":
            arrived[c, 0] = pieces[c, 0]
            grams[c] = [gram_of([arrived[c, flip] for flip in range(owners)])]
            gates.append(grams[c][0])
        elif kind == "apply":
            outs = apply_of(grams[c], [arrived[c, flip] for flip in range(owners)])
            found.update({(c, flip): out for flip, out in enumerate(outs)})
            back[c, 0] = outs[0]
            gates.append(outs[0])
        elif kind == "out":
            back[c, more[0]] = send(found[c, more[0]], more[0])
        elif kind == "weights":
            updated = weights_of((lax.optimization_barrier(tick) - ticks).reshape(1), more[0], c, weights, [back[c, flip] for flip in more[0]], updated)
            gates.append(updated)
        if kind in ("in", "out"):
            tick, ticks = lax.optimization_barrier(tick) + 1, ticks + 1
        if kind == "gram":
            grams[c] += around(grams[c][0], "model")
    return (updated, whole)


def small_body(gradients, momentum, weights):
    new_momentum = hold_rate * momentum + gradients
    stack = lax.all_to_all(new_momentum, "shard", split_axis=0, concat_axis=1, tiled=True)
    gram = mm("mik,mjk->mij", stack, stack)
    gram = gram + sum(around(gram, "model"))
    chain = polynomial(gram, functools.partial(mm, "mij,mjk->mik"))
    back = lax.all_to_all(mm("mij,mjk->mik", chain, stack), "shard", split_axis=1, concat_axis=0, tiled=True)
    return ((1.0 - learn_rate * decay_rate) * weights - learn_rate * back, new_momentum)


def pick(gradients, momentum, weights):
    owners = lax.axis_size("shard")
    mats, rows, columns = gradients.shape
    fits = rows % 8 == 0 and columns % 128 == 0 and mats % (CHUNKS * owners) == 0 and owners & (owners - 1) == 0 and owners // 2 >= FAR
    return (body if fits else small_body)(gradients, momentum, weights)


def solution(mesh):
    placed = P(None, "shard", "model")
    return jax.shard_map(pick, mesh=mesh, in_specs=(placed,) * 3, out_specs=(placed,) * 2, check_vma=False)
```

profile of v0, /device:TPU:1, one launch (start us, length us, event | category | flops | bytes accessed | tf_op | source)
XLA Modules:
  0.0 429.8 jit_solution(16355257670947137605)
XLA Ops:
  14.2 9.2 %collective-permute-done.22.refs_8_.refs_10_ = f32[4,8,2048]{2,1,0:T(8,128)S(1)} collective-permute-done((f32[4,8,2048]{2,1,0:T(8,128)}, f32[4,8,2048]{2,1,0:T(8,128)S(1)}, u32[]{:S(2)}, u32[]{:S(2)}) %collective-permute-start.22) | collective-permute-done | bytes 262176 | tf_op jit(solution)/shard_map/ppermute | solution.py:247
  24.7 7.0 %momentum.6 = (f32[128,8,2048]{2,1,0:T(8,128)}, f32[4,8,2048]{2,1,0:T(8,128)}, f32[4,8,2048]{2,1,0:T(8,128)}, f32[4,8,2048]{2,1,0:T(8,128)}, f32[4,8,2048]{2,1,0...) custom-call(s32[1]{0:T(128)} %bitcast.1.me_ref, ...), custom_call_target="tpu_custom_call", output_to_operand_aliasing={{0}: (3, {})} | custom-call | flops 1048576 | bytes 8388608 | tf_op jit(solution)/shard_map/momentum/pallas_call | solution.py:88
  31.7 13.2 %momentum.7 = (f32[128,8,2048]{2,1,0:T(8,128)}, f32[4,8,2048]{2,1,0:T(8,128)}, f32[4,8,2048]{2,1,0:T(8,128)}, f32[4,8,2048]{2,1,0:T(8,128)}, f32[4,8,2048]{2,1,0...) custom-call(s32[1]{0:T(128)} %bitcast.1.me_ref, ...), custom_call_target="tpu_custom_call", output_to_operand_aliasing={{0}: (3, {})} | custom-call | flops 2097152 | bytes 16777216 | tf_op jit(solution)/shard_map/momentum/pallas_call | solution.py:88
  55.7 23.9 %collective-permute-start.8 = (f32[4,8,2048]{2,1,0:T(8,128)S(1)}, f32[4,8,2048]{2,1,0:T(8,128)S(1)}, u32[]{:S(2)}, u32[]{:S(2)}) collective-permute-start(f32[4,8,2048]{2,1,0:T(8,128)S(1)} %copy-done.60), channel_id=1, source_target_pairs={{0,12},{2,14},{4,8},{6,10},{8,4},{10,6},{12,0},{14,2},{16,28},{18,... | collective-permute-start | bytes 786440 | tf_op jit(solution)/shard_map/ppermute | solution.py:247
  92.5 15.6 %collective-permute-start.11 = (f32[4,8,2048]{2,1,0:T(8,128)}, f32[4,8,2048]{2,1,0:T(8,128)S(1)}, u32[]{:S(2)}, u32[]{:S(2)}) collective-permute-start(f32[4,8,2048]{2,1,0:T(8,128)} %get-tuple-element.144), channel_id=1, source_target_pairs={{0,14},{2,12},{4,10},{6,8},{8,6},{10,4},{12,2},{14,0},{16,30},{18,... | collective-permute-start | bytes 786440 | tf_op jit(solution)/shard_map/ppermute | solution.py:247
  111.3 25.8 %collective-permute-start.17 = (f32[4,8,2048]{2,1,0:T(8,128)}, f32[4,8,2048]{2,1,0:T(8,128)S(1)}, u32[]{:S(2)}, u32[]{:S(2)}) collective-permute-start(f32[4,8,2048]{2,1,0:T(8,128)} %get-tuple-element.153), channel_id=1, source_target_pairs={{0,18},{2,16},{4,22},{6,20},{8,26},{10,24},{12,30},{14,28},{16,2},... | collective-permute-start | bytes 786440 | tf_op jit(solution)/shard_map/ppermute | solution.py:247
  137.1 10.7 %collective-permute-start.15 = (f32[4,8,2048]{2,1,0:T(8,128)}, f32[4,8,2048]{2,1,0:T(8,128)S(1)}, u32[]{:S(2)}, u32[]{:S(2)}) collective-permute-start(f32[4,8,2048]{2,1,0:T(8,128)} %get-tuple-element.150), channel_id=1, source_target_pairs={{0,16},{2,18},{4,20},{6,22},{8,24},{10,26},{12,28},{14,30},{16,0},... | collective-permute-start | bytes 786440 | tf_op jit(solution)/shard_map/ppermute | solution.py:247
  148.7 6.3 %gram.2.refs_0_ = f32[4,128,128]{2,1,0:T(8,128)} custom-call(f32[4,8,2048]{2,1,0:T(8,128)} %get-tuple-element.176.refs_0_.refs_2_, f32[4,8,2048]{2,1,0:T(8,128)} %copy-done.31, f32[4,8,2048]{2,1,0:T(8,128)} %copy-done.36, f32[4,8,2048]{2,1,0:T(8,128)} %copy-done.37, f32[4,8,2048]{2,1,0:T(8,128)} %copy-done.40, f32[4,8,2048]{2,1,0:T(8,128)} %copy-done.49, ...), custom_call_target="tpu_custom_call" | custom-call | flops 1610612736 | bytes 4194304 | tf_op jit(solution)/shard_map/gram/pallas_call | solution.py:145
  177.8 13.9 %apply.2 = (f32[4,8,2048]{2,1,0:T(8,128)}, f32[4,8,2048]{2,1,0:T(8,128)}, f32[4,8,2048]{2,1,0:T(8,128)}, f32[4,8,2048]{2,1,0:T(8,128)}, f32[4,8,2048]{2,1,0:T(8,...) custom-call(f32[4,128,128]{2,1,0:T(8,128)} %gram.2.refs_0_, ...), custom_call_target="tpu_custom_call" | custom-call | flops 2516582400 | bytes 8388608 | tf_op jit(solution)/shard_map/apply/pallas_call | solution.py:171
  198.8 8.6 %collective-permute-start.35 = (f32[4,8,2048]{2,1,0:T(8,128)}, f32[4,8,2048]{2,1,0:T(8,128)S(1)}, u32[]{:S(2)}, u32[]{:S(2)}) collective-permute-start(f32[4,8,2048]{2,1,0:T(8,128)} %get-tuple-element.191), channel_id=1, source_target_pairs={{0,18},{2,16},{4,22},{6,20},{8,26},{10,24},{12,30},{14,28},{16,2},... | collective-permute-start | bytes 786440 | tf_op jit(solution)/shard_map/ppermute | solution.py:247
  207.4 12.1 %collective-permute-start.42 = (f32[4,8,2048]{2,1,0:T(8,128)}, f32[4,8,2048]{2,1,0:T(8,128)S(1)}, u32[]{:S(2)}, u32[]{:S(2)}) collective-permute-start(f32[4,8,2048]{2,1,0:T(8,128)} %get-tuple-element.204), channel_id=1, source_target_pairs={{0,22},{2,20},{4,18},{6,16},{8,30},{10,28},{12,26},{14,24},{16,6},... | collective-permute-start | bytes 786440 | tf_op jit(solution)/shard_map/ppermute | solution.py:247
  227.6 6.3 %gram.3.refs_0_ = f32[4,128,128]{2,1,0:T(8,128)} custom-call(f32[4,8,2048]{2,1,0:T(8,128)} %get-tuple-element.125.refs_0_.refs_2_, f32[4,8,2048]{2,1,0:T(8,128)} %copy-done.38, f32[4,8,2048]{2,1,0:T(8,128)} %copy-done.44, f32[4,8,2048]{2,1,0:T(8,128)} %copy-done.43, f32[4,8,2048]{2,1,0:T(8,128)} %copy-done.42, f32[4,8,2048]{2,1,0:T(8,128)} %copy-done.34, ...), custom_call_target="tpu_custom_call" | custom-call | flops 1610612736 | bytes 4194304 | tf_op jit(solution)/shard_map/gram/pallas_call | solution.py:145
  233.9 23.4 %collective-permute-done.35.refs_3_ = f32[4,8,2048]{2,1,0:T(8,128)S(1)} collective-permute-done((f32[4,8,2048]{2,1,0:T(8,128)}, f32[4,8,2048]{2,1,0:T(8,128)S(1)}, u32[]{:S(2)}, u32[]{:S(2)}) %collective-permute-start.35) | collective-permute-done | bytes 262176 | tf_op jit(solution)/shard_map/ppermute | solution.py:247
  268.6 9.8 %collective-permute-done.38.refs_1_ = f32[4,8,2048]{2,1,0:T(8,128)S(1)} collective-permute-done((f32[4,8,2048]{2,1,0:T(8,128)}, f32[4,8,2048]{2,1,0:T(8,128)S(1)}, u32[]{:S(2)}, u32[]{:S(2)}) %collective-permute-start.38) | collective-permute-done | bytes 262176 | tf_op jit(solution)/shard_map/ppermute | solution.py:247
  284.1 14.0 %apply.3 = (f32[4,8,2048]{2,1,0:T(8,128)}, f32[4,8,2048]{2,1,0:T(8,128)}, f32[4,8,2048]{2,1,0:T(8,128)}, f32[4,8,2048]{2,1,0:T(8,128)}, f32[4,8,2048]{2,1,0:T(8,...) custom-call(f32[4,128,128]{2,1,0:T(8,128)} %gram.3.refs_0_, ...), custom_call_target="tpu_custom_call" | custom-call | flops 2516582400 | bytes 8388608 | tf_op jit(solution)/shard_map/apply/pallas_call | solution.py:171
  305.4 10.9 %collective-permute-done.41.refs_6_ = f32[4,8,2048]{2,1,0:T(8,128)S(1)} collective-permute-done((f32[4,8,2048]{2,1,0:T(8,128)S(1)}, f32[4,8,2048]{2,1,0:T(8,128)S(1)}, u32[]{:S(2)}, u32[]{:S(2)}) %collective-permute-start.41) | collective-permute-done | bytes 262176 | tf_op jit(solution)/shard_map/ppermute | solution.py:247
  316.4 10.3 %collective-permute-start.61 = (f32[4,8,2048]{2,1,0:T(8,128)}, f32[4,8,2048]{2,1,0:T(8,128)S(1)}, u32[]{:S(2)}, u32[]{:S(2)}) collective-permute-start(f32[4,8,2048]{2,1,0:T(8,128)} %get-tuple-element.241), channel_id=1, source_target_pairs={{0,22},{2,20},{4,18},{6,16},{8,30},{10,28},{12,26},{14,24},{16,6},... | collective-permute-start | bytes 786440 | tf_op jit(solution)/shard_map/ppermute | solution.py:247
  332.0 25.2 %collective-permute-done.61.refs_7_ = f32[4,8,2048]{2,1,0:T(8,128)S(1)} collective-permute-done((f32[4,8,2048]{2,1,0:T(8,128)}, f32[4,8,2048]{2,1,0:T(8,128)S(1)}, u32[]{:S(2)}, u32[]{:S(2)}) %collective-permute-start.61) | collective-permute-done | bytes 262176 | tf_op jit(solution)/shard_map/ppermute | solution.py:247
  358.3 9.2 %collective-permute-done.52.refs_3_ = f32[4,8,2048]{2,1,0:T(8,128)S(1)} collective-permute-done((f32[4,8,2048]{2,1,0:T(8,128)}, f32[4,8,2048]{2,1,0:T(8,128)S(1)}, u32[]{:S(2)}, u32[]{:S(2)}) %collective-permute-start.52) | collective-permute-done | bytes 262176 | tf_op jit(solution)/shard_map/ppermute | solution.py:247
  367.5 7.2 %collective-permute-done.50.refs_1_ = f32[4,8,2048]{2,1,0:T(8,128)} collective-permute-done((f32[4,8,2048]{2,1,0:T(8,128)}, f32[4,8,2048]{2,1,0:T(8,128)}, u32[]{:S(2)}, u32[]{:S(2)}) %collective-permute-start.50) | collective-permute-done | bytes 262176 | tf_op jit(solution)/shard_map/ppermute | solution.py:247
  374.9 12.0 %weights.4.refs_8_ = f32[128,8,2048]{2,1,0:T(8,128)} custom-call(s32[1]{0:T(128)} %bitcast.2.me_ref, f32[128,8,2048]{2,1,0:T(8,128)} %weights_ref.7, f32[4,8,2048]{2,1,0:T(8,128)} %get-tuple-element.179.refs_0_, f32[4,8,2048]{2,1,0:T(8,128)} %copy-done.3, f32[4,8,2048]{2,1,0:T(8,128)} %copy-done.4, f32[4,8,2048]{2,1,0:T(8,128)} %copy-done, ...), custom_call_target="tpu_custom_call" | custom-call | flops 3145728 | bytes 12582912 | tf_op jit(solution)/shard_map/weights/pallas_call | solution.py:118
  397.3 6.5 %weights.5.refs_4_ = f32[128,8,2048]{2,1,0:T(8,128)} custom-call(s32[1]{0:T(128)} %bitcast.me_ref, f32[128,8,2048]{2,1,0:T(8,128)} %weights_ref.7, f32[4,8,2048]{2,1,0:T(8,128)} %get-tuple-element.189.refs_0_, f32[4,8,2048]{2,1,0:T(8,128)} %collective-permute-done.50.refs_1_, ...), custom_call_target="tpu_custom_call", output_to_operand_aliasing={{}: (10, {})} | custom-call | flops 1572864 | bytes 6291456 | tf_op jit(solution)/shard_map/weights/pallas_call | solution.py:118
  403.8 9.3 %collective-permute-done.56.refs_2_ = f32[4,8,2048]{2,1,0:T(8,128)S(1)} collective-permute-done((f32[4,8,2048]{2,1,0:T(8,128)}, f32[4,8,2048]{2,1,0:T(8,128)S(1)}, u32[]{:S(2)}, u32[]{:S(2)}) %collective-permute-start.56) | collective-permute-done | bytes 262176 | tf_op jit(solution)/shard_map/ppermute | solution.py:247
  418.9 6.4 %collective-permute-done.51.refs_2_ = f32[4,8,2048]{2,1,0:T(8,128)S(1)} collective-permute-done((f32[4,8,2048]{2,1,0:T(8,128)}, f32[4,8,2048]{2,1,0:T(8,128)S(1)}, u32[]{:S(2)}, u32[]{:S(2)}) %collective-permute-start.51) | collective-permute-done | bytes 262176 | tf_op jit(solution)/shard_map/ppermute | solution.py:247
  (234 shorter events, 131.8 us)
Async XLA Ops:
  5.9 39.0 %collective-permute-start.10 = (f32[4,8,2048]{2,1,0:T(8,128)}, f32[4,8,2048]{2,1,0:T(8,128)S(1)}, u32[]{:S(2)}, u32[]{:S(2)}) collective-permute-start(f32[4,8,2048]{2,1,0:T(8,128)} %get-tuple-element.143), channel_id=1, source_target_pairs={{0,2},{2,0},{4,6},{6,4},{8,10},{10,8},{12,14},{14,12},{16,18},{18,... | collective-permute-start | bytes 786440 | tf_op jit(solution)/shard_map/ppermute | solution.py:247
  12.4 35.9 %collective-permute-start.25 = (f32[4,8,2048]{2,1,0:T(8,128)}, f32[4,8,2048]{2,1,0:T(8,128)S(1)}, u32[]{:S(2)}, u32[]{:S(2)}) collective-permute-start(f32[4,8,2048]{2,1,0:T(8,128)} %get-tuple-element.172), channel_id=1, source_target_pairs={{0,18},{2,16},{4,22},{6,20},{8,26},{10,24},{12,30},{14,28},{16,2},... | collective-permute-start | bytes 786440 | tf_op jit(solution)/shard_map/ppermute | solution.py:247
  12.4 37.5 %collective-permute-start = (f32[4,8,2048]{2,1,0:T(8,128)}, f32[4,8,2048]{2,1,0:T(8,128)S(1)}, u32[]{:S(2)}, u32[]{:S(2)}) collective-permute-start(f32[4,8,2048]{2,1,0:T(8,128)} %get-tuple-element.127), channel_id=1, source_target_pairs={{0,4},{2,6},{4,0},{6,2},{8,12},{10,14},{12,8},{14,10},{16,20},{18,... | collective-permute-start | bytes 786440 | tf_op jit(solution)/shard_map/ppermute | solution.py:247
  13.7 38.0 %collective-permute-start.2 = (f32[4,8,2048]{2,1,0:T(8,128)}, f32[4,8,2048]{2,1,0:T(8,128)S(1)}, u32[]{:S(2)}, u32[]{:S(2)}) collective-permute-start(f32[4,8,2048]{2,1,0:T(8,128)} %get-tuple-element.130), channel_id=1, source_target_pairs={{0,6},{2,4},{4,2},{6,0},{8,14},{10,12},{12,10},{14,8},{16,22},{18,... | collective-permute-start | bytes 786440 | tf_op jit(solution)/shard_map/ppermute | solution.py:247
  48.3 36.7 %collective-permute-start.14 = (f32[4,8,2048]{2,1,0:T(8,128)}, f32[4,8,2048]{2,1,0:T(8,128)S(1)}, u32[]{:S(2)}, u32[]{:S(2)}) collective-permute-start(f32[4,8,2048]{2,1,0:T(8,128)} %get-tuple-element.149), channel_id=1, source_target_pairs={{0,20},{2,22},{4,16},{6,18},{8,28},{10,30},{12,24},{14,26},{16,4},... | collective-permute-start | bytes 786440 | tf_op jit(solution)/shard_map/ppermute | solution.py:247
  49.9 40.7 %collective-permute-start.16 = (f32[4,8,2048]{2,1,0:T(8,128)S(1)}, f32[4,8,2048]{2,1,0:T(8,128)S(1)}, u32[]{:S(2)}, u32[]{:S(2)}) collective-permute-start(f32[4,8,2048]{2,1,0:T(8,128)S(1)} %copy-done.59), channel_id=1, source_target_pairs={{0,22},{2,20},{4,18},{6,16},{8,30},{10,28},{12,26},{14,24},{16,6},... | collective-permute-start | bytes 786440 | tf_op jit(solution)/shard_map/ppermute | solution.py:247
  51.7 40.8 %collective-permute-start.18 = (f32[4,8,2048]{2,1,0:T(8,128)}, f32[4,8,2048]{2,1,0:T(8,128)S(1)}, u32[]{:S(2)}, u32[]{:S(2)}) collective-permute-start(f32[4,8,2048]{2,1,0:T(8,128)} %get-tuple-element.156), channel_id=1, source_target_pairs={{0,24},{2,26},{4,28},{6,30},{8,16},{10,18},{12,20},{14,22},{16,8},... | collective-permute-start | bytes 786440 | tf_op jit(solution)/shard_map/ppermute | solution.py:247
  52.2 55.8 %collective-permute-start.6 = (f32[4,8,2048]{2,1,0:T(8,128)}, f32[4,8,2048]{2,1,0:T(8,128)S(1)}, u32[]{:S(2)}, u32[]{:S(2)}) collective-permute-start(f32[4,8,2048]{2,1,0:T(8,128)} %get-tuple-element.136), channel_id=1, source_target_pairs={{0,10},{2,8},{4,14},{6,12},{8,2},{10,0},{12,6},{14,4},{16,26},{18,... | collective-permute-start | bytes 786440 | tf_op jit(solution)/shard_map/ppermute | solution.py:247
  55.7 53.1 %collective-permute-start.8 = (f32[4,8,2048]{2,1,0:T(8,128)S(1)}, f32[4,8,2048]{2,1,0:T(8,128)S(1)}, u32[]{:S(2)}, u32[]{:S(2)}) collective-permute-start(f32[4,8,2048]{2,1,0:T(8,128)S(1)} %copy-done.60), channel_id=1, source_target_pairs={{0,12},{2,14},{4,8},{6,10},{8,4},{10,6},{12,0},{14,2},{16,28},{18,... | collective-permute-start | bytes 786440 | tf_op jit(solution)/shard_map/ppermute | solution.py:247
  90.6 46.5 %collective-permute-start.23 = (f32[4,8,2048]{2,1,0:T(8,128)}, f32[4,8,2048]{2,1,0:T(8,128)S(1)}, u32[]{:S(2)}, u32[]{:S(2)}) collective-permute-start(f32[4,8,2048]{2,1,0:T(8,128)} %get-tuple-element.167), channel_id=1, source_target_pairs={{0,28},{2,30},{4,24},{6,26},{8,20},{10,22},{12,16},{14,18},{16,12}... | collective-permute-start | bytes 786440 | tf_op jit(solution)/shard_map/ppermute | solution.py:247
  92.5 55.3 %collective-permute-start.11 = (f32[4,8,2048]{2,1,0:T(8,128)}, f32[4,8,2048]{2,1,0:T(8,128)S(1)}, u32[]{:S(2)}, u32[]{:S(2)}) collective-permute-start(f32[4,8,2048]{2,1,0:T(8,128)} %get-tuple-element.144), channel_id=1, source_target_pairs={{0,14},{2,12},{4,10},{6,8},{8,6},{10,4},{12,2},{14,0},{16,30},{18,... | collective-permute-start | bytes 786440 | tf_op jit(solution)/shard_map/ppermute | solution.py:247
  108.0 39.9 %collective-permute-start.21 = (f32[4,8,2048]{2,1,0:T(8,128)}, f32[4,8,2048]{2,1,0:T(8,128)S(1)}, u32[]{:S(2)}, u32[]{:S(2)}) collective-permute-start(f32[4,8,2048]{2,1,0:T(8,128)} %get-tuple-element.162), channel_id=1, source_target_pairs={{0,22},{2,20},{4,18},{6,16},{8,30},{10,28},{12,26},{14,24},{16,6},... | collective-permute-start | bytes 786440 | tf_op jit(solution)/shard_map/ppermute | solution.py:247
  108.8 49.1 %collective-permute-start.19 = (f32[4,8,2048]{2,1,0:T(8,128)}, f32[4,8,2048]{2,1,0:T(8,128)S(1)}, u32[]{:S(2)}, u32[]{:S(2)}) collective-permute-start(f32[4,8,2048]{2,1,0:T(8,128)} %get-tuple-element.157), channel_id=1, source_target_pairs={{0,20},{2,22},{4,16},{6,18},{8,28},{10,30},{12,24},{14,26},{16,4},... | collective-permute-start | bytes 786440 | tf_op jit(solution)/shard_map/ppermute | solution.py:247
  111.3 51.2 %collective-permute-start.17 = (f32[4,8,2048]{2,1,0:T(8,128)}, f32[4,8,2048]{2,1,0:T(8,128)S(1)}, u32[]{:S(2)}, u32[]{:S(2)}) collective-permute-start(f32[4,8,2048]{2,1,0:T(8,128)} %get-tuple-element.153), channel_id=1, source_target_pairs={{0,18},{2,16},{4,22},{6,20},{8,26},{10,24},{12,30},{14,28},{16,2},... | collective-permute-start | bytes 786440 | tf_op jit(solution)/shard_map/ppermute | solution.py:247
  198.8 58.5 %collective-permute-start.35 = (f32[4,8,2048]{2,1,0:T(8,128)}, f32[4,8,2048]{2,1,0:T(8,128)S(1)}, u32[]{:S(2)}, u32[]{:S(2)}) collective-permute-start(f32[4,8,2048]{2,1,0:T(8,128)} %get-tuple-element.191), channel_id=1, source_target_pairs={{0,18},{2,16},{4,22},{6,20},{8,26},{10,24},{12,30},{14,28},{16,2},... | collective-permute-start | bytes 786440 | tf_op jit(solution)/shard_map/ppermute | solution.py:247
  207.4 55.2 %collective-permute-start.42 = (f32[4,8,2048]{2,1,0:T(8,128)}, f32[4,8,2048]{2,1,0:T(8,128)S(1)}, u32[]{:S(2)}, u32[]{:S(2)}) collective-permute-start(f32[4,8,2048]{2,1,0:T(8,128)} %get-tuple-element.204), channel_id=1, source_target_pairs={{0,22},{2,20},{4,18},{6,16},{8,30},{10,28},{12,26},{14,24},{16,6},... | collective-permute-start | bytes 786440 | tf_op jit(solution)/shard_map/ppermute | solution.py:247
  219.5 48.6 %collective-permute-start.40 = (f32[4,8,2048]{2,1,0:T(8,128)}, f32[4,8,2048]{2,1,0:T(8,128)S(1)}, u32[]{:S(2)}, u32[]{:S(2)}) collective-permute-start(f32[4,8,2048]{2,1,0:T(8,128)} %get-tuple-element.200), channel_id=1, source_target_pairs={{0,20},{2,22},{4,16},{6,18},{8,28},{10,30},{12,24},{14,26},{16,4},... | collective-permute-start | bytes 786440 | tf_op jit(solution)/shard_map/ppermute | solution.py:247
  219.6 58.8 %collective-permute-start.38 = (f32[4,8,2048]{2,1,0:T(8,128)}, f32[4,8,2048]{2,1,0:T(8,128)S(1)}, u32[]{:S(2)}, u32[]{:S(2)}) collective-permute-start(f32[4,8,2048]{2,1,0:T(8,128)} %get-tuple-element.196), channel_id=1, source_target_pairs={{0,16},{2,18},{4,20},{6,22},{8,24},{10,26},{12,28},{14,30},{16,0},... | collective-permute-start | bytes 786440 | tf_op jit(solution)/shard_map/ppermute | solution.py:247
  226.8 52.6 %collective-permute-start.39 = (f32[4,8,2048]{2,1,0:T(8,128)}, f32[4,8,2048]{2,1,0:T(8,128)S(1)}, u32[]{:S(2)}, u32[]{:S(2)}) collective-permute-start(f32[4,8,2048]{2,1,0:T(8,128)} %get-tuple-element.198), channel_id=1, source_target_pairs={{0,2},{2,0},{4,6},{6,4},{8,10},{10,8},{12,14},{14,12},{16,18},{18,... | collective-permute-start | bytes 786440 | tf_op jit(solution)/shard_map/ppermute | solution.py:247
  262.6 35.5 %collective-permute-start.44 = (f32[4,8,2048]{2,1,0:T(8,128)}, f32[4,8,2048]{2,1,0:T(8,128)S(1)}, u32[]{:S(2)}, u32[]{:S(2)}) collective-permute-start(f32[4,8,2048]{2,1,0:T(8,128)} %get-tuple-element.208), channel_id=1, source_target_pairs={{0,24},{2,26},{4,28},{6,30},{8,16},{10,18},{12,20},{14,22},{16,8},... | collective-permute-start | bytes 786440 | tf_op jit(solution)/shard_map/ppermute | solution.py:247
  316.4 40.8 %collective-permute-start.61 = (f32[4,8,2048]{2,1,0:T(8,128)}, f32[4,8,2048]{2,1,0:T(8,128)S(1)}, u32[]{:S(2)}, u32[]{:S(2)}) collective-permute-start(f32[4,8,2048]{2,1,0:T(8,128)} %get-tuple-element.241), channel_id=1, source_target_pairs={{0,22},{2,20},{4,18},{6,16},{8,30},{10,28},{12,26},{14,24},{16,6},... | collective-permute-start | bytes 786440 | tf_op jit(solution)/shard_map/ppermute | solution.py:247
  326.8 40.7 %collective-permute-start.52 = (f32[4,8,2048]{2,1,0:T(8,128)}, f32[4,8,2048]{2,1,0:T(8,128)S(1)}, u32[]{:S(2)}, u32[]{:S(2)}) collective-permute-start(f32[4,8,2048]{2,1,0:T(8,128)} %get-tuple-element.224), channel_id=1, source_target_pairs={{0,18},{2,16},{4,22},{6,20},{8,26},{10,24},{12,30},{14,28},{16,2},... | collective-permute-start | bytes 786440 | tf_op jit(solution)/shard_map/ppermute | solution.py:247
  327.5 47.2 %collective-permute-start.50 = (f32[4,8,2048]{2,1,0:T(8,128)}, f32[4,8,2048]{2,1,0:T(8,128)}, u32[]{:S(2)}, u32[]{:S(2)}) collective-permute-start(f32[4,8,2048]{2,1,0:T(8,128)} %get-tuple-element.220), channel_id=1, source_target_pairs={{0,16},{2,18},{4,20},{6,22},{8,24},{10,26},{12,28},{14,30},{16,0},... | collective-permute-start | bytes 786440 | tf_op jit(solution)/shard_map/ppermute | solution.py:247
  332.0 42.7 %collective-permute-start.33 = (f32[4,8,2048]{2,1,0:T(8,128)}, f32[4,8,2048]{2,1,0:T(8,128)}, u32[]{:S(2)}, u32[]{:S(2)}) collective-permute-start(f32[4,8,2048]{2,1,0:T(8,128)} %get-tuple-element.185), channel_id=1, source_target_pairs={{0,2},{2,0},{4,6},{6,4},{8,10},{10,8},{12,14},{14,12},{16,18},{18,... | collective-permute-start | bytes 786440 | tf_op jit(solution)/shard_map/ppermute | solution.py:247
  (99 other events, 4450.0 us)
where the time goes:
time: 434 us; the launch traced here: 430 us
  starting transfers between devices  178 us (41%)
  waiting for transfers between devices  154 us (35%)
  Pallas kernels  94.2 us (22%)
    ppermute x60, starting transfers between devices, send(): lax.ppermute(piece, 'shard', [(i, i ^ flip) for i in range(owners)])  175 us
    ppermute x60, waiting for transfers between devices, send(): lax.ppermute(piece, 'shard', [(i, i ^ flip) for i in range(owners)])  154 us
    pallas_call x2, Pallas kernels, apply_of(): pl.pallas_call(functools.partial(apply_kernel, len(grams), len(pieces)),...  27.9 us
    pallas_call x4, Pallas kernels, momentum_of(): pl.pallas_call(functools.partial(momentum_kernel, count), grid_spec=pltpu...  27.8 us
    pallas_call x4, Pallas kernels, weights_of(): pl.pallas_call(functools.partial(weights_kernel, count), grid_spec=pltpu....  26 us
    pallas_call x2, Pallas kernels, gram_of(): pl.pallas_call(gram_kernel, grid=(held,), in_specs=[pl.BlockSpec((1, rows...  12.6 us
  transfers between devices with their start and end apart: 62, of which 22 were waited for; matrix products, arithmetic and copies ran while one was open for 0% of the time, Pallas kernels for 21%

commit v1 on v0

--- a/solution.py
+++ b/solution.py
@@ -13,9 +13,10 @@
 FAR = 6
 NEAR = 6
 LATER = 1
-HEAD = (2, 6)
+HEAD = (1, 3, 4)
 TAIL = 3
-LAST = (8, 4)
+LAST = (8, 4, 3)
+VMEM = 52 << 20
 
 hold_rate = 0.9
 learn_rate = 0.9
@@ -108,11 +109,11 @@
             refs[-1][...] = (1.0 - learn_rate * decay_rate) * weights_ref[...] - learn_rate * refs[k][...]
 
 
-def weights_of(me, flips, chunk, weights, back, whole):
+def weights_of(me, flips, chunk, weights, back, whole, landed):
     _, rows, columns = weights.shape
     count, held = len(flips), back[0].shape[0]
     there = places(flips, held, rows, columns, chunk)
-    here = pl.BlockSpec((held, rows, columns), lambda i, me: (0, 0, 0))
+    here = pl.BlockSpec(memory_space=pltpu.VMEM) if landed else pl.BlockSpec((held, rows, columns), lambda i, me: (0, 0, 0))
     size = count * held * rows * columns
     more = [] if whole is None else [whole]
     return pl.pallas_call(
@@ -125,6 +126,7 @@
         ),
         out_shape=jax.ShapeDtypeStruct(weights.shape, jnp.float32),
         input_output_aliases={2 + count: 0} if more else {},
+        compiler_params=pltpu.CompilerParams(vmem_limit_bytes=VMEM),
         cost_estimate=cost(3 * size, 12 * size),
         name="weights",
     )(me, weights, *back, *more)
@@ -266,7 +268,7 @@
         elif kind == "out":
             back[c, more[0]] = send(found[c, more[0]], more[0])
         elif kind == "weights":
-            updated = weights_of((lax.optimization_barrier(tick) - ticks).reshape(1), more[0], c, weights, [back[c, flip] for flip in more[0]], updated)
+            updated = weights_of((lax.optimization_barrier(tick) - ticks).reshape(1), more[0], c, weights, [back[c, flip] for flip in more[0]], updated, len(more[0]) < owners // 2)
             gates.append(updated)
         if kind in ("in", "out"):
             tick, ticks = lax.optimization_barrier(tick) + 1, ticks + 1

time: 434 us -> 425 us (0.979)
  waiting for transfers between devices: 154 us -> 147 us
    ppermute x60, waiting for transfers between devices: 154 us -> 147 us  [send(): lax.ppermute(piece, 'shard', [(i, i ^ flip) for i in range(owners)])]
    pallas_call x4 -> x5, Pallas kernels: 27.8 us -> 29.3 us  [momentum_of(): pl.pallas_call(functools.partial(momentum_kernel, count), grid_spec=pltpu...]
    pallas_call x4 -> x5, Pallas kernels: 26 us -> 25.6 us  [weights_of(): pl.pallas_call(functools.partial(weights_kernel, count), grid_spec=pltpu....]
  transfers between devices with their start and end apart: 62 -> 62, of which waited for: 22 -> 23; matrix products, arithmetic and copies ran while one was open for 0% -> 0% of each run, Pallas kernels for 21% -> 22%
where the time goes in v1:
time: 425 us; the launch traced here: 420 us
  starting transfers between devices  175 us (41%)
  waiting for transfers between devices  147 us (35%)
  Pallas kernels  95.3 us (22%)
    ppermute x60, starting transfers between devices, send(): lax.ppermute(piece, 'shard', [(i, i ^ flip) for i in range(owners)])  174 us
    ppermute x60, waiting for transfers between devices, send(): lax.ppermute(piece, 'shard', [(i, i ^ flip) for i in range(owners)])  147 us
    pallas_call x5, Pallas kernels, momentum_of(): pl.pallas_call(functools.partial(momentum_kernel, count), grid_spec=pltpu...  29.3 us
    pallas_call x2, Pallas kernels, apply_of(): pl.pallas_call(functools.partial(apply_kernel, len(grams), len(pieces)),...  27.8 us
    pallas_call x5, Pallas kernels, weights_of(): pl.pallas_call(functools.partial(weights_kernel, count), grid_spec=pltpu....  25.6 us
    pallas_call x2, Pallas kernels, gram_of(): pl.pallas_call(gram_kernel, grid=(held,), in_specs=[pl.BlockSpec((1, rows...  12.5 us
  transfers between devices with their start and end apart: 62, of which 23 were waited for; matrix products, arithmetic and copies ran while one was open for 0% of the time, Pallas kernels for 22%

profile of v1, /device:TPU:1, one launch (start us, length us, event | category | flops | bytes accessed | tf_op | source)
XLA Modules:
  0.0 419.6 jit_solution(14682377239323522358)
XLA Ops:
  17.8 10.9 %collective-permute-done.22.refs_8_.refs_10_ = f32[4,8,2048]{2,1,0:T(8,128)S(1)} collective-permute-done((f32[4,8,2048]{2,1,0:T(8,128)}, f32[4,8,2048]{2,1,0:T(8,128)S(1)}, u32[]{:S(2)}, u32[]{:S(2)}) %collective-permute-start.22) | collective-permute-done | bytes 262176 | tf_op jit(solution)/shard_map/ppermute | solution.py:249
  32.2 6.9 %momentum.8 = (f32[128,8,2048]{2,1,0:T(8,128)}, f32[4,8,2048]{2,1,0:T(8,128)}, f32[4,8,2048]{2,1,0:T(8,128)}, f32[4,8,2048]{2,1,0:T(8,128)}, f32[4,8,2048]{2,1,0...) custom-call(s32[1]{0:T(128)} %bitcast.1.me_ref, ...), custom_call_target="tpu_custom_call", output_to_operand_aliasing={{0}: (3, {})} | custom-call | flops 1048576 | bytes 8388608 | tf_op jit(solution)/shard_map/momentum/pallas_call | solution.py:89
  39.2 13.1 %momentum.9 = (f32[128,8,2048]{2,1,0:T(8,128)}, f32[4,8,2048]{2,1,0:T(8,128)}, f32[4,8,2048]{2,1,0:T(8,128)}, f32[4,8,2048]{2,1,0:T(8,128)}, f32[4,8,2048]{2,1,0...) custom-call(s32[1]{0:T(128)} %bitcast.1.me_ref, ...), custom_call_target="tpu_custom_call", output_to_operand_aliasing={{0}: (3, {})} | custom-call | flops 2097152 | bytes 16777216 | tf_op jit(solution)/shard_map/momentum/pallas_call | solution.py:89
  74.5 8.5 %collective-permute-done.16.refs_11_.refs_13_ = f32[4,8,2048]{2,1,0:T(8,128)S(1)} collective-permute-done((f32[4,8,2048]{2,1,0:T(8,128)}, f32[4,8,2048]{2,1,0:T(8,128)S(1)}, u32[]{:S(2)}, u32[]{:S(2)}) %collective-permute-start.16) | collective-permute-done | bytes 262176 | tf_op jit(solution)/shard_map/ppermute | solution.py:249
  91.4 6.8 %collective-permute-done.26.refs_15_.refs_17_ = f32[4,8,2048]{2,1,0:T(8,128)S(1)} collective-permute-done((f32[4,8,2048]{2,1,0:T(8,128)}, f32[4,8,2048]{2,1,0:T(8,128)S(1)}, u32[]{:S(2)}, u32[]{:S(2)}) %collective-permute-start.26) | collective-permute-done | bytes 262176 | tf_op jit(solution)/shard_map/ppermute | solution.py:249
  98.2 29.2 %collective-permute-start.17 = (f32[4,8,2048]{2,1,0:T(8,128)}, f32[4,8,2048]{2,1,0:T(8,128)S(1)}, u32[]{:S(2)}, u32[]{:S(2)}) collective-permute-start(f32[4,8,2048]{2,1,0:T(8,128)} %get-tuple-element.158), channel_id=1, source_target_pairs={{0,18},{2,16},{4,22},{6,20},{8,26},{10,24},{12,30},{14,28},{16,2},... | collective-permute-start | bytes 786440 | tf_op jit(solution)/shard_map/ppermute | solution.py:249
  127.4 11.9 %collective-permute-start.15 = (f32[4,8,2048]{2,1,0:T(8,128)}, f32[4,8,2048]{2,1,0:T(8,128)S(1)}, u32[]{:S(2)}, u32[]{:S(2)}) collective-permute-start(f32[4,8,2048]{2,1,0:T(8,128)} %get-tuple-element.155), channel_id=1, source_target_pairs={{0,16},{2,18},{4,20},{6,22},{8,24},{10,26},{12,28},{14,30},{16,0},... | collective-permute-start | bytes 786440 | tf_op jit(solution)/shard_map/ppermute | solution.py:249
  139.3 6.1 %collective-permute-done.21.refs_11_.refs_13_ = f32[4,8,2048]{2,1,0:T(8,128)S(1)} collective-permute-done((f32[4,8,2048]{2,1,0:T(8,128)}, f32[4,8,2048]{2,1,0:T(8,128)S(1)}, u32[]{:S(2)}, u32[]{:S(2)}) %collective-permute-start.21) | collective-permute-done | bytes 262176 | tf_op jit(solution)/shard_map/ppermute | solution.py:249
  145.5 6.3 %gram.2.refs_0_ = f32[4,128,128]{2,1,0:T(8,128)} custom-call(f32[4,8,2048]{2,1,0:T(8,128)} %get-tuple-element.180.refs_0_.refs_2_, f32[4,8,2048]{2,1,0:T(8,128)} %copy-done.21, f32[4,8,2048]{2,1,0:T(8,128)} %copy-done.22, f32[4,8,2048]{2,1,0:T(8,128)} %copy-done.27, f32[4,8,2048]{2,1,0:T(8,128)} %copy-done.32, f32[4,8,2048]{2,1,0:T(8,128)} %copy-done.35, ...), custom_call_target="tpu_custom_call" | custom-call | flops 1610612736 | bytes 4194304 | tf_op jit(solution)/shard_map/gram/pallas_call | solution.py:147
  170.3 13.9 %apply.2 = (f32[4,8,2048]{2,1,0:T(8,128)}, f32[4,8,2048]{2,1,0:T(8,128)}, f32[4,8,2048]{2,1,0:T(8,128)}, f32[4,8,2048]{2,1,0:T(8,128)}, f32[4,8,2048]{2,1,0:T(8,...) custom-call(f32[4,128,128]{2,1,0:T(8,128)} %gram.2.refs_0_, ...), custom_call_target="tpu_custom_call" | custom-call | flops 2516582400 | bytes 8388608 | tf_op jit(solution)/shard_map/apply/pallas_call | solution.py:173
  191.2 7.9 %collective-permute-start.38 = (f32[4,8,2048]{2,1,0:T(8,128)}, f32[4,8,2048]{2,1,0:T(8,128)S(1)}, u32[]{:S(2)}, u32[]{:S(2)}) collective-permute-start(f32[4,8,2048]{2,1,0:T(8,128)} %get-tuple-element.201), channel_id=1, source_target_pairs={{0,18},{2,16},{4,22},{6,20},{8,26},{10,24},{12,30},{14,28},{16,2},... | collective-permute-start | bytes 786440 | tf_op jit(solution)/shard_map/ppermute | solution.py:249
  199.2 12.7 %collective-permute-start.32 = (f32[4,8,2048]{2,1,0:T(8,128)}, f32[4,8,2048]{2,1,0:T(8,128)S(1)}, u32[]{:S(2)}, u32[]{:S(2)}) collective-permute-start(f32[4,8,2048]{2,1,0:T(8,128)} %get-tuple-element.188), channel_id=1, source_target_pairs={{0,22},{2,20},{4,18},{6,16},{8,30},{10,28},{12,26},{14,24},{16,6},... | collective-permute-start | bytes 786440 | tf_op jit(solution)/shard_map/ppermute | solution.py:249
  221.2 6.3 %gram.3.refs_0_ = f32[4,128,128]{2,1,0:T(8,128)} custom-call(f32[4,8,2048]{2,1,0:T(8,128)} %get-tuple-element.128.refs_0_.refs_2_, f32[4,8,2048]{2,1,0:T(8,128)} %collective-permute-done.1.refs_1_.refs_3_, f32[4,8,2048]{2,1,0:T(8,128)} %copy-done.30, f32[4,8,2048]{2,1,0:T(8,128)} %copy-done.29, f32[4,8,2048]{2,1,0:T(8,128)} %copy-done.28, ...), custom_call_target="tpu_custom_call" | custom-call | flops 1610612736 | bytes 4194304 | tf_op jit(solution)/shard_map/gram/pallas_call | solution.py:147
  227.5 23.3 %collective-permute-done.38.refs_3_ = f32[4,8,2048]{2,1,0:T(8,128)S(1)} collective-permute-done((f32[4,8,2048]{2,1,0:T(8,128)}, f32[4,8,2048]{2,1,0:T(8,128)S(1)}, u32[]{:S(2)}, u32[]{:S(2)}) %collective-permute-start.38) | collective-permute-done | bytes 262176 | tf_op jit(solution)/shard_map/ppermute | solution.py:249
  265.8 6.7 %collective-permute-done.41.refs_1_ = f32[4,8,2048]{2,1,0:T(8,128)S(1)} collective-permute-done((f32[4,8,2048]{2,1,0:T(8,128)}, f32[4,8,2048]{2,1,0:T(8,128)S(1)}, u32[]{:S(2)}, u32[]{:S(2)}) %collective-permute-start.41) | collective-permute-done | bytes 262176 | tf_op jit(solution)/shard_map/ppermute | solution.py:249
  274.7 13.9 %apply.3 = (f32[4,8,2048]{2,1,0:T(8,128)}, f32[4,8,2048]{2,1,0:T(8,128)}, f32[4,8,2048]{2,1,0:T(8,128)}, f32[4,8,2048]{2,1,0:T(8,128)}, f32[4,8,2048]{2,1,0:T(8,...) custom-call(f32[4,128,128]{2,1,0:T(8,128)} %gram.3.refs_0_, ...), custom_call_target="tpu_custom_call" | custom-call | flops 2516582400 | bytes 8388608 | tf_op jit(solution)/shard_map/apply/pallas_call | solution.py:173
  297.2 11.0 %collective-permute-done.44.refs_6_ = f32[4,8,2048]{2,1,0:T(8,128)S(1)} collective-permute-done((f32[4,8,2048]{2,1,0:T(8,128)}, f32[4,8,2048]{2,1,0:T(8,128)S(1)}, u32[]{:S(2)}, u32[]{:S(2)}) %collective-permute-start.44) | collective-permute-done | bytes 262176 | tf_op jit(solution)/shard_map/ppermute | solution.py:249
  308.2 11.2 %collective-permute-start.61 = (f32[4,8,2048]{2,1,0:T(8,128)}, f32[4,8,2048]{2,1,0:T(8,128)S(1)}, u32[]{:S(2)}, u32[]{:S(2)}) collective-permute-start(f32[4,8,2048]{2,1,0:T(8,128)} %get-tuple-element.245), channel_id=1, source_target_pairs={{0,22},{2,20},{4,18},{6,16},{8,30},{10,28},{12,26},{14,24},{16,6},... | collective-permute-start | bytes 786440 | tf_op jit(solution)/shard_map/ppermute | solution.py:249
  322.1 19.0 %collective-permute-start.33 = (f32[4,8,2048]{2,1,0:T(8,128)}, f32[4,8,2048]{2,1,0:T(8,128)S(1)}, u32[]{:S(2)}, u32[]{:S(2)}) collective-permute-start(f32[4,8,2048]{2,1,0:T(8,128)} %get-tuple-element.189), channel_id=1, source_target_pairs={{0,18},{2,16},{4,22},{6,20},{8,26},{10,24},{12,30},{14,28},{16,2},... | collective-permute-start | bytes 786440 | tf_op jit(solution)/shard_map/ppermute | solution.py:249
  341.1 7.4 %collective-permute-done.61.refs_7_ = f32[4,8,2048]{2,1,0:T(8,128)S(1)} collective-permute-done((f32[4,8,2048]{2,1,0:T(8,128)}, f32[4,8,2048]{2,1,0:T(8,128)S(1)}, u32[]{:S(2)}, u32[]{:S(2)}) %collective-permute-start.61) | collective-permute-done | bytes 262176 | tf_op jit(solution)/shard_map/ppermute | solution.py:249
  350.4 9.4 %collective-permute-done.52.refs_1_ = f32[4,8,2048]{2,1,0:T(8,128)S(1)} collective-permute-done((f32[4,8,2048]{2,1,0:T(8,128)}, f32[4,8,2048]{2,1,0:T(8,128)S(1)}, u32[]{:S(2)}, u32[]{:S(2)}) %collective-permute-start.52) | collective-permute-done | bytes 262176 | tf_op jit(solution)/shard_map/ppermute | solution.py:249
  366.5 11.3 %weights.5.refs_8_ = f32[128,8,2048]{2,1,0:T(8,128)} custom-call(s32[1]{0:T(128)} %bitcast.2.me_ref, f32[128,8,2048]{2,1,0:T(8,128)} %weights_ref.9, f32[4,8,2048]{2,1,0:T(8,128)S(1)} %copy-done, f32[4,8,2048]{2,1,0:T(8,128)S(1)} %collective-permute-done.41.refs_1_, f32[4,8,2048]{2,1,0:T(8,128)S(1)} %collective-permute-done.42.refs_2_, ...), custom_call_target="tpu_custom_call" | custom-call | flops 3145728 | bytes 12582912 | tf_op jit(solution)/shard_map/weights/pallas_call | solution.py:119
  385.4 8.4 %collective-permute-done.54.refs_0_ = f32[4,8,2048]{2,1,0:T(8,128)} collective-permute-done((f32[4,8,2048]{2,1,0:T(8,128)}, f32[4,8,2048]{2,1,0:T(8,128)}, u32[]{:S(2)}, u32[]{:S(2)}) %collective-permute-start.54) | collective-permute-done | bytes 262176 | tf_op jit(solution)/shard_map/ppermute | solution.py:249
  407.2 7.7 %collective-permute-done.37.refs_0_ = f32[4,8,2048]{2,1,0:T(8,128)S(1)} collective-permute-done((f32[4,8,2048]{2,1,0:T(8,128)}, f32[4,8,2048]{2,1,0:T(8,128)S(1)}, u32[]{:S(2)}, u32[]{:S(2)}) %collective-permute-start.37) | collective-permute-done | bytes 262176 | tf_op jit(solution)/shard_map/ppermute | solution.py:249
  (208 shorter events, 148.5 us)
Async XLA Ops:
  9.0 43.4 %collective-permute-start.10 = (f32[4,8,2048]{2,1,0:T(8,128)}, f32[4,8,2048]{2,1,0:T(8,128)S(1)}, u32[]{:S(2)}, u32[]{:S(2)}) collective-permute-start(f32[4,8,2048]{2,1,0:T(8,128)} %get-tuple-element.147), channel_id=1, source_target_pairs={{0,2},{2,0},{4,6},{6,4},{8,10},{10,8},{12,14},{14,12},{16,18},{18,... | collective-permute-start | bytes 786440 | tf_op jit(solution)/shard_map/ppermute | solution.py:249
  10.0 44.5 %collective-permute-start = (f32[4,8,2048]{2,1,0:T(8,128)}, f32[4,8,2048]{2,1,0:T(8,128)S(1)}, u32[]{:S(2)}, u32[]{:S(2)}) collective-permute-start(f32[4,8,2048]{2,1,0:T(8,128)} %get-tuple-element.130), channel_id=1, source_target_pairs={{0,4},{2,6},{4,0},{6,2},{8,12},{10,14},{12,8},{14,10},{16,20},{18,... | collective-permute-start | bytes 786440 | tf_op jit(solution)/shard_map/ppermute | solution.py:249
  11.2 43.3 %collective-permute-start.25 = (f32[4,8,2048]{2,1,0:T(8,128)}, f32[4,8,2048]{2,1,0:T(8,128)S(1)}, u32[]{:S(2)}, u32[]{:S(2)}) collective-permute-start(f32[4,8,2048]{2,1,0:T(8,128)} %get-tuple-element.176), channel_id=1, source_target_pairs={{0,18},{2,16},{4,22},{6,20},{8,26},{10,24},{12,30},{14,28},{16,2},... | collective-permute-start | bytes 786440 | tf_op jit(solution)/shard_map/ppermute | solution.py:249
  15.5 40.7 %collective-permute-start.14 = (f32[4,8,2048]{2,1,0:T(8,128)}, f32[4,8,2048]{2,1,0:T(8,128)S(1)}, u32[]{:S(2)}, u32[]{:S(2)}) collective-permute-start(f32[4,8,2048]{2,1,0:T(8,128)} %get-tuple-element.154), channel_id=1, source_target_pairs={{0,20},{2,22},{4,16},{6,18},{8,28},{10,30},{12,24},{14,26},{16,4},... | collective-permute-start | bytes 786440 | tf_op jit(solution)/shard_map/ppermute | solution.py:249
  58.7 30.7 %collective-permute-start.6 = (f32[4,8,2048]{2,1,0:T(8,128)}, f32[4,8,2048]{2,1,0:T(8,128)S(1)}, u32[]{:S(2)}, u32[]{:S(2)}) collective-permute-start(f32[4,8,2048]{2,1,0:T(8,128)} %get-tuple-element.139), channel_id=1, source_target_pairs={{0,10},{2,8},{4,14},{6,12},{8,2},{10,0},{12,6},{14,4},{16,26},{18,... | collective-permute-start | bytes 786440 | tf_op jit(solution)/shard_map/ppermute | solution.py:249
  83.0 44.4 %collective-permute-start.23 = (f32[4,8,2048]{2,1,0:T(8,128)}, f32[4,8,2048]{2,1,0:T(8,128)S(1)}, u32[]{:S(2)}, u32[]{:S(2)}) collective-permute-start(f32[4,8,2048]{2,1,0:T(8,128)} %get-tuple-element.172), channel_id=1, source_target_pairs={{0,28},{2,30},{4,24},{6,26},{8,20},{10,22},{12,16},{14,18},{16,12}... | collective-permute-start | bytes 786440 | tf_op jit(solution)/shard_map/ppermute | solution.py:249
  84.9 54.3 %collective-permute-start.11 = (f32[4,8,2048]{2,1,0:T(8,128)}, f32[4,8,2048]{2,1,0:T(8,128)S(1)}, u32[]{:S(2)}, u32[]{:S(2)}) collective-permute-start(f32[4,8,2048]{2,1,0:T(8,128)} %get-tuple-element.148), channel_id=1, source_target_pairs={{0,14},{2,12},{4,10},{6,8},{8,6},{10,4},{12,2},{14,0},{16,30},{18,... | collective-permute-start | bytes 786440 | tf_op jit(solution)/shard_map/ppermute | solution.py:249
  89.4 56.0 %collective-permute-start.21 = (f32[4,8,2048]{2,1,0:T(8,128)}, f32[4,8,2048]{2,1,0:T(8,128)S(1)}, u32[]{:S(2)}, u32[]{:S(2)}) collective-permute-start(f32[4,8,2048]{2,1,0:T(8,128)} %get-tuple-element.167), channel_id=1, source_target_pairs={{0,22},{2,20},{4,18},{6,16},{8,30},{10,28},{12,26},{14,24},{16,6},... | collective-permute-start | bytes 786440 | tf_op jit(solution)/shard_map/ppermute | solution.py:249
  90.7 61.1 %collective-permute-start.19 = (f32[4,8,2048]{2,1,0:T(8,128)}, f32[4,8,2048]{2,1,0:T(8,128)S(1)}, u32[]{:S(2)}, u32[]{:S(2)}) collective-permute-start(f32[4,8,2048]{2,1,0:T(8,128)} %get-tuple-element.162), channel_id=1, source_target_pairs={{0,20},{2,22},{4,16},{6,18},{8,28},{10,30},{12,24},{14,26},{16,4},... | collective-permute-start | bytes 786440 | tf_op jit(solution)/shard_map/ppermute | solution.py:249
  98.2 57.6 %collective-permute-start.17 = (f32[4,8,2048]{2,1,0:T(8,128)}, f32[4,8,2048]{2,1,0:T(8,128)S(1)}, u32[]{:S(2)}, u32[]{:S(2)}) collective-permute-start(f32[4,8,2048]{2,1,0:T(8,128)} %get-tuple-element.158), channel_id=1, source_target_pairs={{0,18},{2,16},{4,22},{6,20},{8,26},{10,24},{12,30},{14,28},{16,2},... | collective-permute-start | bytes 786440 | tf_op jit(solution)/shard_map/ppermute | solution.py:249
  127.4 32.7 %collective-permute-start.15 = (f32[4,8,2048]{2,1,0:T(8,128)}, f32[4,8,2048]{2,1,0:T(8,128)S(1)}, u32[]{:S(2)}, u32[]{:S(2)}) collective-permute-start(f32[4,8,2048]{2,1,0:T(8,128)} %get-tuple-element.155), channel_id=1, source_target_pairs={{0,16},{2,18},{4,20},{6,22},{8,24},{10,26},{12,28},{14,30},{16,0},... | collective-permute-start | bytes 786440 | tf_op jit(solution)/shard_map/ppermute | solution.py:249
  188.9 31.5 %collective-permute-start.30 = (f32[4,8,2048]{2,1,0:T(8,128)S(1)}, f32[4,8,2048]{2,1,0:T(8,128)S(1)}, u32[]{:S(2)}, u32[]{:S(2)}) collective-permute-start(f32[4,8,2048]{2,1,0:T(8,128)S(1)} %copy-done.12), channel_id=1, source_target_pairs={{0,30},{2,28},{4,26},{6,24},{8,22},{10,20},{12,18},{14,16},{16,14}... | collective-permute-start | bytes 786440 | tf_op jit(solution)/shard_map/ppermute | solution.py:249
  191.2 59.5 %collective-permute-start.38 = (f32[4,8,2048]{2,1,0:T(8,128)}, f32[4,8,2048]{2,1,0:T(8,128)S(1)}, u32[]{:S(2)}, u32[]{:S(2)}) collective-permute-start(f32[4,8,2048]{2,1,0:T(8,128)} %get-tuple-element.201), channel_id=1, source_target_pairs={{0,18},{2,16},{4,22},{6,20},{8,26},{10,24},{12,30},{14,28},{16,2},... | collective-permute-start | bytes 786440 | tf_op jit(solution)/shard_map/ppermute | solution.py:249
  199.2 56.7 %collective-permute-start.32 = (f32[4,8,2048]{2,1,0:T(8,128)}, f32[4,8,2048]{2,1,0:T(8,128)S(1)}, u32[]{:S(2)}, u32[]{:S(2)}) collective-permute-start(f32[4,8,2048]{2,1,0:T(8,128)} %get-tuple-element.188), channel_id=1, source_target_pairs={{0,22},{2,20},{4,18},{6,16},{8,30},{10,28},{12,26},{14,24},{16,6},... | collective-permute-start | bytes 786440 | tf_op jit(solution)/shard_map/ppermute | solution.py:249
  211.9 49.6 %collective-permute-start.43 = (f32[4,8,2048]{2,1,0:T(8,128)}, f32[4,8,2048]{2,1,0:T(8,128)S(1)}, u32[]{:S(2)}, u32[]{:S(2)}) collective-permute-start(f32[4,8,2048]{2,1,0:T(8,128)} %get-tuple-element.210), channel_id=1, source_target_pairs={{0,20},{2,22},{4,16},{6,18},{8,28},{10,30},{12,24},{14,26},{16,4},... | collective-permute-start | bytes 786440 | tf_op jit(solution)/shard_map/ppermute | solution.py:249
  211.9 60.5 %collective-permute-start.41 = (f32[4,8,2048]{2,1,0:T(8,128)}, f32[4,8,2048]{2,1,0:T(8,128)S(1)}, u32[]{:S(2)}, u32[]{:S(2)}) collective-permute-start(f32[4,8,2048]{2,1,0:T(8,128)} %get-tuple-element.206), channel_id=1, source_target_pairs={{0,16},{2,18},{4,20},{6,22},{8,24},{10,26},{12,28},{14,30},{16,0},... | collective-permute-start | bytes 786440 | tf_op jit(solution)/shard_map/ppermute | solution.py:249
  220.5 52.0 %collective-permute-start.42 = (f32[4,8,2048]{2,1,0:T(8,128)}, f32[4,8,2048]{2,1,0:T(8,128)S(1)}, u32[]{:S(2)}, u32[]{:S(2)}) collective-permute-start(f32[4,8,2048]{2,1,0:T(8,128)} %get-tuple-element.208), channel_id=1, source_target_pairs={{0,2},{2,0},{4,6},{6,4},{8,10},{10,8},{12,14},{14,12},{16,18},{18,... | collective-permute-start | bytes 786440 | tf_op jit(solution)/shard_map/ppermute | solution.py:249
  255.8 32.8 %collective-permute-start.46 = (f32[4,8,2048]{2,1,0:T(8,128)}, f32[4,8,2048]{2,1,0:T(8,128)S(1)}, u32[]{:S(2)}, u32[]{:S(2)}) collective-permute-start(f32[4,8,2048]{2,1,0:T(8,128)} %get-tuple-element.216), channel_id=1, source_target_pairs={{0,24},{2,26},{4,28},{6,30},{8,16},{10,18},{12,20},{14,22},{16,8},... | collective-permute-start | bytes 786440 | tf_op jit(solution)/shard_map/ppermute | solution.py:249
  308.2 40.3 %collective-permute-start.61 = (f32[4,8,2048]{2,1,0:T(8,128)}, f32[4,8,2048]{2,1,0:T(8,128)S(1)}, u32[]{:S(2)}, u32[]{:S(2)}) collective-permute-start(f32[4,8,2048]{2,1,0:T(8,128)} %get-tuple-element.245), channel_id=1, source_target_pairs={{0,22},{2,20},{4,18},{6,16},{8,30},{10,28},{12,26},{14,24},{16,6},... | collective-permute-start | bytes 786440 | tf_op jit(solution)/shard_map/ppermute | solution.py:249
  321.6 38.2 %collective-permute-start.52 = (f32[4,8,2048]{2,1,0:T(8,128)}, f32[4,8,2048]{2,1,0:T(8,128)S(1)}, u32[]{:S(2)}, u32[]{:S(2)}) collective-permute-start(f32[4,8,2048]{2,1,0:T(8,128)} %get-tuple-element.228), channel_id=1, source_target_pairs={{0,16},{2,18},{4,20},{6,22},{8,24},{10,26},{12,28},{14,30},{16,0},... | collective-permute-start | bytes 786440 | tf_op jit(solution)/shard_map/ppermute | solution.py:249
  321.7 39.8 %collective-permute-start.36 = (f32[4,8,2048]{2,1,0:T(8,128)}, f32[4,8,2048]{2,1,0:T(8,128)S(1)}, u32[]{:S(2)}, u32[]{:S(2)}) collective-permute-start(f32[4,8,2048]{2,1,0:T(8,128)} %get-tuple-element.195), channel_id=1, source_target_pairs={{0,2},{2,0},{4,6},{6,4},{8,10},{10,8},{12,14},{14,12},{16,18},{18,... | collective-permute-start | bytes 786440 | tf_op jit(solution)/shard_map/ppermute | solution.py:249
  322.1 44.2 %collective-permute-start.33 = (f32[4,8,2048]{2,1,0:T(8,128)}, f32[4,8,2048]{2,1,0:T(8,128)S(1)}, u32[]{:S(2)}, u32[]{:S(2)}) collective-permute-start(f32[4,8,2048]{2,1,0:T(8,128)} %get-tuple-element.189), channel_id=1, source_target_pairs={{0,18},{2,16},{4,22},{6,20},{8,26},{10,24},{12,30},{14,28},{16,2},... | collective-permute-start | bytes 786440 | tf_op jit(solution)/shard_map/ppermute | solution.py:249
  381.3 33.6 %collective-permute-start.37 = (f32[4,8,2048]{2,1,0:T(8,128)}, f32[4,8,2048]{2,1,0:T(8,128)S(1)}, u32[]{:S(2)}, u32[]{:S(2)}) collective-permute-start(f32[4,8,2048]{2,1,0:T(8,128)} %get-tuple-element.196), channel_id=1, source_target_pairs={{0,14},{2,12},{4,10},{6,8},{8,6},{10,4},{12,2},{14,0},{16,30},{18,... | collective-permute-start | bytes 786440 | tf_op jit(solution)/shard_map/ppermute | solution.py:249
  383.8 31.2 %collective-permute-start.53 = (f32[4,8,2048]{2,1,0:T(8,128)}, f32[4,8,2048]{2,1,0:T(8,128)S(1)}, u32[]{:S(2)}, u32[]{:S(2)}) collective-permute-start(f32[4,8,2048]{2,1,0:T(8,128)} %get-tuple-element.229), channel_id=1, source_target_pairs={{0,28},{2,30},{4,24},{6,26},{8,20},{10,22},{12,16},{14,18},{16,12}... | collective-permute-start | bytes 786440 | tf_op jit(solution)/shard_map/ppermute | solution.py:249
  (85 other events, 3437.3 us)

commit v2 on v1

--- a/solution.py
+++ b/solution.py
@@ -15,7 +15,8 @@
 LATER = 1
 HEAD = (1, 3, 4)
 TAIL = 3
-LAST = (8, 4, 3)
+LAST = (8, 4)
+LEAD = 1
 VMEM = 52 << 20
 
 hold_rate = 0.9
@@ -130,6 +131,52 @@
         cost_estimate=cost(3 * size, 12 * size),
         name="weights",
     )(me, weights, *back, *more)
+
+
+def ahead_kernel(me_ref, weights_ref, out_ref):
+    out_ref[...] = (1.0 - learn_rate * decay_rate) * weights_ref[...]
+
+
+def close_kernel(me_ref, ready_ref, back_ref, _, out_ref):
+    out_ref[...] = ready_ref[...] - learn_rate * back_ref[...]
+
+
+def ahead_of(me, flip, chunk, held, weights):
+    _, rows, columns = weights.shape
+    size = held * rows * columns
+    return pl.pallas_call(
+        ahead_kernel,
+        grid_spec=pltpu.PrefetchScalarGridSpec(
+            num_scalar_prefetch=1,
+            grid=(1,),
+            in_specs=[places((flip,), held, rows, columns, chunk)],
+            out_specs=pl.BlockSpec((held, rows, columns), lambda i, me: (0, 0, 0)),
+        ),
+        out_shape=jax.ShapeDtypeStruct((held, rows, columns), jnp.float32),
+        compiler_params=pltpu.CompilerParams(vmem_limit_bytes=VMEM),
+        cost_estimate=cost(size, 8 * size),
+        name="ahead",
+    )(me, weights)
+
+
+def close_of(me, flip, chunk, ready, back, whole):
+    held, rows, columns = back.shape
+    size = held * rows * columns
+    near = pl.BlockSpec(memory_space=pltpu.VMEM)
+    return pl.pallas_call(
+        close_kernel,
+        grid_spec=pltpu.PrefetchScalarGridSpec(
+            num_scalar_prefetch=1,
+            grid=(1,),
+            in_specs=[near, near, pl.BlockSpec(memory_space=pl.ANY)],
+            out_specs=places((flip,), held, rows, columns, chunk),
+        ),
+        out_shape=jax.ShapeDtypeStruct(whole.shape, jnp.float32),
+        input_output_aliases={3: 0},
+        compiler_params=pltpu.CompilerParams(vmem_limit_bytes=VMEM),
+        cost_estimate=cost(2 * size, 12 * size),
+        name="close",
+    )(me, ready, back, whole)
 
 
 def stacked(refs):
@@ -211,12 +258,14 @@
             due.append((half * (CHUNKS + c + 1) + FAR, ("weights", c, tuple([0] + flips))))
     due.sort(key=lambda one: one[0])
     steps, gone = [], 0
-    heads = cut(flips + [0], HEAD)
+    first = woven(far[half // 2:half // 2 + LEAD] + far[:half // 2] + far[half // 2 + LEAD:], near)
+    heads = cut(first + [0], HEAD)
     steps.append(("momentum", 0, heads[0]))
     rest, ready = heads[1:], set(heads[0])
     for kind in ("in", "out"):
         for c in range(CHUNKS):
             order = flips if (kind, c) != ("out", CHUNKS - 1) else woven(far[:-TAIL], near) + far[-TAIL:]
+            order = first if (kind, c) == ("in", 0) else order
             for flip in order:
                 while kind == "in" and c == 0 and flip not in ready:
                     steps.append(("momentum", 0, rest[0]))
@@ -226,7 +275,9 @@
                 steps.append((kind, c, flip))
                 gone += flip in far
     steps += [one for _, one in due]
-    return steps + [("weights", CHUNKS - 1, run) for run in cut([0] + order, LAST)]
+    steps.append(("ahead", CHUNKS - 1, order[-1]))
+    steps += [("weights", CHUNKS - 1, run) for run in cut([0] + order[:-1], LAST)]
+    return steps + [("close", CHUNKS - 1, order[-1])]
 
 
 def body(gradients, momentum, weights):
@@ -270,6 +321,10 @@
         elif kind == "weights":
             updated = weights_of((lax.optimization_barrier(tick) - ticks).reshape(1), more[0], c, weights, [back[c, flip] for flip in more[0]], updated, len(more[0]) < owners // 2)
             gates.append(updated)
+        elif kind == "ahead":
+            ready = ahead_of(me, more[0], c, held, weights)
+        elif kind == "close":
+            updated = close_of(me, more[0], c, ready, back[c, more[0]], updated)
         if kind in ("in", "out"):
             tick, ticks = lax.optimization_barrier(tick) + 1, ticks + 1
         if kind == "gram":

time: 425 us -> 417 us (0.981)
  waiting for transfers between devices: 147 us -> 118 us
  starting transfers between devices: 175 us -> 199 us
    ppermute x60, waiting for transfers between devices: 147 us -> 118 us  [send(): lax.ppermute(piece, 'shard', [(i, i ^ flip) for i in range(owners)])]
    ppermute x60, starting transfers between devices: 174 us -> 196 us  [send(): lax.ppermute(piece, 'shard', [(i, i ^ flip) for i in range(owners)])]
    pallas_call x5 -> x4, Pallas kernels: 25.6 us -> 23.8 us  [weights_of(): pl.pallas_call(functools.partial(weights_kernel, count), grid_spec=pltpu....]
  transfers between devices with their start and end apart: 62 -> 62, of which waited for: 23 -> 19; matrix products, arithmetic and copies ran while one was open for 0% -> 0% of each run, Pallas kernels for 22% -> 22%
where the time goes in v2:
time: 417 us; the launch traced here: 415 us
  starting transfers between devices  199 us (48%)
  waiting for transfers between devices  118 us (28%)
  Pallas kernels  95.3 us (23%)
    ppermute x60, starting transfers between devices, send(): lax.ppermute(piece, 'shard', [(i, i ^ flip) for i in range(owners)])  196 us
    ppermute x60, waiting for transfers between devices, send(): lax.ppermute(piece, 'shard', [(i, i ^ flip) for i in range(owners)])  118 us
    pallas_call x5, Pallas kernels, momentum_of(): pl.pallas_call(functools.partial(momentum_kernel, count), grid_spec=pltpu...  29.4 us
    pallas_call x2, Pallas kernels, apply_of(): pl.pallas_call(functools.partial(apply_kernel, len(grams), len(pieces)),...  27.9 us
    pallas_call x4, Pallas kernels, weights_of(): pl.pallas_call(functools.partial(weights_kernel, count), grid_spec=pltpu....  23.8 us
    pallas_call x2, Pallas kernels, gram_of(): pl.pallas_call(gram_kernel, grid=(held,), in_specs=[pl.BlockSpec((1, rows...  12.5 us
  transfers between devices with their start and end apart: 62, of which 19 were waited for; matrix products, arithmetic and copies ran while one was open for 0% of the time, Pallas kernels for 22%

profile of v2, /device:TPU:1, one launch (start us, length us, event | category | flops | bytes accessed | tf_op | source)
XLA Modules:
  0.0 414.7 jit_solution(10223384440143647988)
XLA Ops:
  19.1 7.0 %momentum.8 = (f32[128,8,2048]{2,1,0:T(8,128)}, f32[4,8,2048]{2,1,0:T(8,128)}, f32[4,8,2048]{2,1,0:T(8,128)}, f32[4,8,2048]{2,1,0:T(8,128)}, f32[4,8,2048]{2,1,0...) custom-call(s32[1]{0:T(128)} %bitcast.me_ref, ...), custom_call_target="tpu_custom_call", output_to_operand_aliasing={{0}: (3, {})} | custom-call | flops 1048576 | bytes 8388608 | tf_op jit(solution)/shard_map/momentum/pallas_call | solution.py:90
  26.1 13.1 %momentum.9 = (f32[128,8,2048]{2,1,0:T(8,128)}, f32[4,8,2048]{2,1,0:T(8,128)}, f32[4,8,2048]{2,1,0:T(8,128)}, f32[4,8,2048]{2,1,0:T(8,128)}, f32[4,8,2048]{2,1,0...) custom-call(s32[1]{0:T(128)} %bitcast.me_ref, ...), custom_call_target="tpu_custom_call", output_to_operand_aliasing={{0}: (3, {})} | custom-call | flops 2097152 | bytes 16777216 | tf_op jit(solution)/shard_map/momentum/pallas_call | solution.py:90
  39.6 13.6 %collective-permute-start.4 = (f32[4,8,2048]{2,1,0:T(8,128)S(1)}, f32[4,8,2048]{2,1,0:T(8,128)S(1)}, u32[]{:S(2)}, u32[]{:S(2)}) collective-permute-start(f32[4,8,2048]{2,1,0:T(8,128)S(1)} %copy-done.48), channel_id=1, source_target_pairs={{0,8},{2,10},{4,12},{6,14},{8,0},{10,2},{12,4},{14,6},{16,24},{18,... | collective-permute-start | bytes 786440 | tf_op jit(solution)/shard_map/ppermute | solution.py:300
  63.6 13.7 %collective-permute-done.16.refs_10_.refs_12_ = f32[4,8,2048]{2,1,0:T(8,128)S(1)} collective-permute-done((f32[4,8,2048]{2,1,0:T(8,128)}, f32[4,8,2048]{2,1,0:T(8,128)S(1)}, u32[]{:S(2)}, u32[]{:S(2)}) %collective-permute-start.16) | collective-permute-done | bytes 262176 | tf_op jit(solution)/shard_map/ppermute | solution.py:300
  90.8 14.1 %collective-permute-start.17 = (f32[4,8,2048]{2,1,0:T(8,128)}, f32[4,8,2048]{2,1,0:T(8,128)S(1)}, u32[]{:S(2)}, u32[]{:S(2)}) collective-permute-start(f32[4,8,2048]{2,1,0:T(8,128)} %get-tuple-element.158), channel_id=1, source_target_pairs={{0,18},{2,16},{4,22},{6,20},{8,26},{10,24},{12,30},{14,28},{16,2},... | collective-permute-start | bytes 786440 | tf_op jit(solution)/shard_map/ppermute | solution.py:300
  104.9 17.3 %collective-permute-start.15 = (f32[4,8,2048]{2,1,0:T(8,128)}, f32[4,8,2048]{2,1,0:T(8,128)S(1)}, u32[]{:S(2)}, u32[]{:S(2)}) collective-permute-start(f32[4,8,2048]{2,1,0:T(8,128)} %get-tuple-element.155), channel_id=1, source_target_pairs={{0,16},{2,18},{4,20},{6,22},{8,24},{10,26},{12,28},{14,30},{16,0},... | collective-permute-start | bytes 786440 | tf_op jit(solution)/shard_map/ppermute | solution.py:300
  122.2 12.9 %collective-permute-start.9 = (f32[4,8,2048]{2,1,0:T(8,128)}, f32[4,8,2048]{2,1,0:T(8,128)S(1)}, u32[]{:S(2)}, u32[]{:S(2)}) collective-permute-start(f32[4,8,2048]{2,1,0:T(8,128)} %get-tuple-element.143), channel_id=1, source_target_pairs={{0,10},{2,8},{4,14},{6,12},{8,2},{10,0},{12,6},{14,4},{16,26},{18,... | collective-permute-start | bytes 786440 | tf_op jit(solution)/shard_map/ppermute | solution.py:300
  140.0 6.3 %gram.2.refs_0_ = f32[4,128,128]{2,1,0:T(8,128)} custom-call(f32[4,8,2048]{2,1,0:T(8,128)} %get-tuple-element.180.refs_0_.refs_2_, f32[4,8,2048]{2,1,0:T(8,128)} %copy-done.21, f32[4,8,2048]{2,1,0:T(8,128)} %copy-done.22, f32[4,8,2048]{2,1,0:T(8,128)} %copy-done.29, f32[4,8,2048]{2,1,0:T(8,128)} %copy-done.34, f32[4,8,2048]{2,1,0:T(8,128)} %copy-done.37, ...), custom_call_target="tpu_custom_call" | custom-call | flops 1610612736 | bytes 4194304 | tf_op jit(solution)/shard_map/gram/pallas_call | solution.py:194
  166.2 14.0 %apply.2 = (f32[4,8,2048]{2,1,0:T(8,128)}, f32[4,8,2048]{2,1,0:T(8,128)}, f32[4,8,2048]{2,1,0:T(8,128)}, f32[4,8,2048]{2,1,0:T(8,128)}, f32[4,8,2048]{2,1,0:T(8,...) custom-call(f32[4,128,128]{2,1,0:T(8,128)} %gram.2.refs_0_, ...), custom_call_target="tpu_custom_call" | custom-call | flops 2516582400 | bytes 8388608 | tf_op jit(solution)/shard_map/apply/pallas_call | solution.py:220
  187.3 6.3 %collective-permute-start.38 = (f32[4,8,2048]{2,1,0:T(8,128)}, f32[4,8,2048]{2,1,0:T(8,128)S(1)}, u32[]{:S(2)}, u32[]{:S(2)}) collective-permute-start(f32[4,8,2048]{2,1,0:T(8,128)} %get-tuple-element.201), channel_id=1, source_target_pairs={{0,18},{2,16},{4,22},{6,20},{8,26},{10,24},{12,30},{14,28},{16,2},... | collective-permute-start | bytes 786440 | tf_op jit(solution)/shard_map/ppermute | solution.py:300
  193.5 12.6 %collective-permute-start.32 = (f32[4,8,2048]{2,1,0:T(8,128)}, f32[4,8,2048]{2,1,0:T(8,128)S(1)}, u32[]{:S(2)}, u32[]{:S(2)}) collective-permute-start(f32[4,8,2048]{2,1,0:T(8,128)} %get-tuple-element.188), channel_id=1, source_target_pairs={{0,22},{2,20},{4,18},{6,16},{8,30},{10,28},{12,26},{14,24},{16,6},... | collective-permute-start | bytes 786440 | tf_op jit(solution)/shard_map/ppermute | solution.py:300
  217.7 6.3 %gram.3.refs_0_ = f32[4,128,128]{2,1,0:T(8,128)} custom-call(f32[4,8,2048]{2,1,0:T(8,128)} %get-tuple-element.128.refs_0_.refs_2_, f32[4,8,2048]{2,1,0:T(8,128)} %copy-done.28, f32[4,8,2048]{2,1,0:T(8,128)} %copy-done.32, f32[4,8,2048]{2,1,0:T(8,128)} %copy-done.31, f32[4,8,2048]{2,1,0:T(8,128)} %copy-done.30, f32[4,8,2048]{2,1,0:T(8,128)} %copy-done.26, ...), custom_call_target="tpu_custom_call" | custom-call | flops 1610612736 | bytes 4194304 | tf_op jit(solution)/shard_map/gram/pallas_call | solution.py:194
  224.0 21.2 %collective-permute-done.38.refs_3_ = f32[4,8,2048]{2,1,0:T(8,128)S(1)} collective-permute-done((f32[4,8,2048]{2,1,0:T(8,128)}, f32[4,8,2048]{2,1,0:T(8,128)S(1)}, u32[]{:S(2)}, u32[]{:S(2)}) %collective-permute-start.38) | collective-permute-done | bytes 262176 | tf_op jit(solution)/shard_map/ppermute | solution.py:300
  251.3 10.6 %collective-permute-done.43.refs_5_ = f32[4,8,2048]{2,1,0:T(8,128)S(1)} collective-permute-done((f32[4,8,2048]{2,1,0:T(8,128)}, f32[4,8,2048]{2,1,0:T(8,128)S(1)}, u32[]{:S(2)}, u32[]{:S(2)}) %collective-permute-start.43) | collective-permute-done | bytes 262176 | tf_op jit(solution)/shard_map/ppermute | solution.py:300
  270.2 13.9 %apply.3 = (f32[4,8,2048]{2,1,0:T(8,128)}, f32[4,8,2048]{2,1,0:T(8,128)}, f32[4,8,2048]{2,1,0:T(8,128)}, f32[4,8,2048]{2,1,0:T(8,128)}, f32[4,8,2048]{2,1,0:T(8,...) custom-call(f32[4,128,128]{2,1,0:T(8,128)} %gram.3.refs_0_, ...), custom_call_target="tpu_custom_call" | custom-call | flops 2516582400 | bytes 8388608 | tf_op jit(solution)/shard_map/apply/pallas_call | solution.py:220
  291.9 11.7 %collective-permute-done.44.refs_6_ = f32[4,8,2048]{2,1,0:T(8,128)S(1)} collective-permute-done((f32[4,8,2048]{2,1,0:T(8,128)}, f32[4,8,2048]{2,1,0:T(8,128)S(1)}, u32[]{:S(2)}, u32[]{:S(2)}) %collective-permute-start.44) | collective-permute-done | bytes 262176 | tf_op jit(solution)/shard_map/ppermute | solution.py:300
  303.6 11.0 %collective-permute-start.61 = (f32[4,8,2048]{2,1,0:T(8,128)}, f32[4,8,2048]{2,1,0:T(8,128)S(1)}, u32[]{:S(2)}, u32[]{:S(2)}) collective-permute-start(f32[4,8,2048]{2,1,0:T(8,128)} %get-tuple-element.245), channel_id=1, source_target_pairs={{0,22},{2,20},{4,18},{6,16},{8,30},{10,28},{12,26},{14,24},{16,6},... | collective-permute-start | bytes 786440 | tf_op jit(solution)/shard_map/ppermute | solution.py:300
  318.9 16.0 %collective-permute-start.33 = (f32[4,8,2048]{2,1,0:T(8,128)}, f32[4,8,2048]{2,1,0:T(8,128)S(1)}, u32[]{:S(2)}, u32[]{:S(2)}) collective-permute-start(f32[4,8,2048]{2,1,0:T(8,128)} %get-tuple-element.189), channel_id=1, source_target_pairs={{0,18},{2,16},{4,22},{6,20},{8,26},{10,24},{12,30},{14,28},{16,2},... | collective-permute-start | bytes 786440 | tf_op jit(solution)/shard_map/ppermute | solution.py:300
  335.0 9.3 %collective-permute-done.61.refs_7_ = f32[4,8,2048]{2,1,0:T(8,128)S(1)} collective-permute-done((f32[4,8,2048]{2,1,0:T(8,128)}, f32[4,8,2048]{2,1,0:T(8,128)S(1)}, u32[]{:S(2)}, u32[]{:S(2)}) %collective-permute-start.61) | collective-permute-done | bytes 262176 | tf_op jit(solution)/shard_map/ppermute | solution.py:300
  346.4 8.9 %collective-permute-start.57 = (f32[4,8,2048]{2,1,0:T(8,128)}, f32[4,8,2048]{2,1,0:T(8,128)}, u32[]{:S(2)}, u32[]{:S(2)}) collective-permute-start(f32[4,8,2048]{2,1,0:T(8,128)} %get-tuple-element.237), channel_id=1, source_target_pairs={{0,12},{2,14},{4,8},{6,10},{8,4},{10,6},{12,0},{14,2},{16,28},{18,... | collective-permute-start | bytes 786440 | tf_op jit(solution)/shard_map/ppermute | solution.py:300
  361.2 11.2 %weights.4.refs_8_ = f32[128,8,2048]{2,1,0:T(8,128)} custom-call(s32[1]{0:T(128)} %bitcast.2.me_ref, f32[128,8,2048]{2,1,0:T(8,128)} %weights_ref.9, f32[4,8,2048]{2,1,0:T(8,128)S(1)} %copy-done, f32[4,8,2048]{2,1,0:T(8,128)S(1)} %collective-permute-done.41.refs_1_, f32[4,8,2048]{2,1,0:T(8,128)S(1)} %collective-permute-done.42.refs_2_, ...), custom_call_target="tpu_custom_call" | custom-call | flops 3145728 | bytes 12582912 | tf_op jit(solution)/shard_map/weights/pallas_call | solution.py:120
  381.4 10.8 %collective-permute-start.34 = (f32[4,8,2048]{2,1,0:T(8,128)}, f32[4,8,2048]{2,1,0:T(8,128)S(1)}, u32[]{:S(2)}, u32[]{:S(2)}) collective-permute-start(f32[4,8,2048]{2,1,0:T(8,128)} %get-tuple-element.190), channel_id=1, source_target_pairs={{0,30},{2,28},{4,26},{6,24},{8,22},{10,20},{12,18},{14,16},{16,14}... | collective-permute-start | bytes 786440 | tf_op jit(solution)/shard_map/ppermute | solution.py:300
  393.2 5.9 %weights.5.refs_4_ = f32[128,8,2048]{2,1,0:T(8,128)} custom-call(s32[1]{0:T(128)} %bitcast.1.me_ref, f32[128,8,2048]{2,1,0:T(8,128)} %weights_ref.9, f32[4,8,2048]{2,1,0:T(8,128)S(1)} %copy-done.1, f32[4,8,2048]{2,1,0:T(8,128)S(1)} %collective-permute-done.52.refs_1_, ...), custom_call_target="tpu_custom_call", output_to_operand_aliasing={{}: (10, {})} | custom-call | flops 1572864 | bytes 6291456 | tf_op jit(solution)/shard_map/weights/pallas_call | solution.py:120
  402.8 8.2 %collective-permute-done.37.refs_0_ = f32[4,8,2048]{2,1,0:T(8,128)S(1)} collective-permute-done((f32[4,8,2048]{2,1,0:T(8,128)}, f32[4,8,2048]{2,1,0:T(8,128)S(1)}, u32[]{:S(2)}, u32[]{:S(2)}) %collective-permute-start.37) | collective-permute-done | bytes 262176 | tf_op jit(solution)/shard_map/ppermute | solution.py:300
  (215 shorter events, 137.7 us)
Async XLA Ops:
  12.2 40.9 %collective-permute-start.25 = (f32[4,8,2048]{2,1,0:T(8,128)}, f32[4,8,2048]{2,1,0:T(8,128)S(1)}, u32[]{:S(2)}, u32[]{:S(2)}) collective-permute-start(f32[4,8,2048]{2,1,0:T(8,128)} %get-tuple-element.176), channel_id=1, source_target_pairs={{0,16},{2,18},{4,20},{6,22},{8,24},{10,26},{12,28},{14,30},{16,0},... | collective-permute-start | bytes 786440 | tf_op jit(solution)/shard_map/ppermute | solution.py:300
  16.2 37.9 %collective-permute-start.14 = (f32[4,8,2048]{2,1,0:T(8,128)}, f32[4,8,2048]{2,1,0:T(8,128)S(1)}, u32[]{:S(2)}, u32[]{:S(2)}) collective-permute-start(f32[4,8,2048]{2,1,0:T(8,128)} %get-tuple-element.154), channel_id=1, source_target_pairs={{0,18},{2,16},{4,22},{6,20},{8,26},{10,24},{12,30},{14,28},{16,2},... | collective-permute-start | bytes 786440 | tf_op jit(solution)/shard_map/ppermute | solution.py:300
  19.1 39.3 %collective-permute-start.2 = (f32[4,8,2048]{2,1,0:T(8,128)}, f32[4,8,2048]{2,1,0:T(8,128)S(1)}, u32[]{:S(2)}, u32[]{:S(2)}) collective-permute-start(f32[4,8,2048]{2,1,0:T(8,128)} %get-tuple-element.133), channel_id=1, source_target_pairs={{0,6},{2,4},{4,2},{6,0},{8,14},{10,12},{12,10},{14,8},{16,22},{18,... | collective-permute-start | bytes 786440 | tf_op jit(solution)/shard_map/ppermute | solution.py:300
  84.2 38.1 %collective-permute-start.11 = (f32[4,8,2048]{2,1,0:T(8,128)}, f32[4,8,2048]{2,1,0:T(8,128)S(1)}, u32[]{:S(2)}, u32[]{:S(2)}) collective-permute-start(f32[4,8,2048]{2,1,0:T(8,128)} %get-tuple-element.148), channel_id=1, source_target_pairs={{0,14},{2,12},{4,10},{6,8},{8,6},{10,4},{12,2},{14,0},{16,30},{18,... | collective-permute-start | bytes 786440 | tf_op jit(solution)/shard_map/ppermute | solution.py:300
  84.2 55.7 %collective-permute-start.21 = (f32[4,8,2048]{2,1,0:T(8,128)}, f32[4,8,2048]{2,1,0:T(8,128)S(1)}, u32[]{:S(2)}, u32[]{:S(2)}) collective-permute-start(f32[4,8,2048]{2,1,0:T(8,128)} %get-tuple-element.167), channel_id=1, source_target_pairs={{0,22},{2,20},{4,18},{6,16},{8,30},{10,28},{12,26},{14,24},{16,6},... | collective-permute-start | bytes 786440 | tf_op jit(solution)/shard_map/ppermute | solution.py:300
  88.4 57.8 %collective-permute-start.19 = (f32[4,8,2048]{2,1,0:T(8,128)}, f32[4,8,2048]{2,1,0:T(8,128)S(1)}, u32[]{:S(2)}, u32[]{:S(2)}) collective-permute-start(f32[4,8,2048]{2,1,0:T(8,128)} %get-tuple-element.162), channel_id=1, source_target_pairs={{0,20},{2,22},{4,16},{6,18},{8,28},{10,30},{12,24},{14,26},{16,4},... | collective-permute-start | bytes 786440 | tf_op jit(solution)/shard_map/ppermute | solution.py:300
  90.8 58.3 %collective-permute-start.17 = (f32[4,8,2048]{2,1,0:T(8,128)}, f32[4,8,2048]{2,1,0:T(8,128)S(1)}, u32[]{:S(2)}, u32[]{:S(2)}) collective-permute-start(f32[4,8,2048]{2,1,0:T(8,128)} %get-tuple-element.158), channel_id=1, source_target_pairs={{0,18},{2,16},{4,22},{6,20},{8,26},{10,24},{12,30},{14,28},{16,2},... | collective-permute-start | bytes 786440 | tf_op jit(solution)/shard_map/ppermute | solution.py:300
  104.9 49.1 %collective-permute-start.15 = (f32[4,8,2048]{2,1,0:T(8,128)}, f32[4,8,2048]{2,1,0:T(8,128)S(1)}, u32[]{:S(2)}, u32[]{:S(2)}) collective-permute-start(f32[4,8,2048]{2,1,0:T(8,128)} %get-tuple-element.155), channel_id=1, source_target_pairs={{0,16},{2,18},{4,20},{6,22},{8,24},{10,26},{12,28},{14,30},{16,0},... | collective-permute-start | bytes 786440 | tf_op jit(solution)/shard_map/ppermute | solution.py:300
  122.2 34.8 %collective-permute-start.9 = (f32[4,8,2048]{2,1,0:T(8,128)}, f32[4,8,2048]{2,1,0:T(8,128)S(1)}, u32[]{:S(2)}, u32[]{:S(2)}) collective-permute-start(f32[4,8,2048]{2,1,0:T(8,128)} %get-tuple-element.143), channel_id=1, source_target_pairs={{0,10},{2,8},{4,14},{6,12},{8,2},{10,0},{12,6},{14,4},{16,26},{18,... | collective-permute-start | bytes 786440 | tf_op jit(solution)/shard_map/ppermute | solution.py:300
  149.1 31.1 %collective-permute-start.7 = (f32[4,8,2048]{2,1,0:T(8,128)}, f32[4,8,2048]{2,1,0:T(8,128)S(1)}, u32[]{:S(2)}, u32[]{:S(2)}) collective-permute-start(f32[4,8,2048]{2,1,0:T(8,128)} %get-tuple-element.140), channel_id=1, source_target_pairs={{0,8},{2,10},{4,12},{6,14},{8,0},{10,2},{12,4},{14,6},{16,24},{18,... | collective-permute-start | bytes 786440 | tf_op jit(solution)/shard_map/ppermute | solution.py:300
  184.2 32.8 %collective-permute-start.30 = (f32[4,8,2048]{2,1,0:T(8,128)S(1)}, f32[4,8,2048]{2,1,0:T(8,128)S(1)}, u32[]{:S(2)}, u32[]{:S(2)}) collective-permute-start(f32[4,8,2048]{2,1,0:T(8,128)S(1)} %copy-done.12), channel_id=1, source_target_pairs={{0,30},{2,28},{4,26},{6,24},{8,22},{10,20},{12,18},{14,16},{16,14}... | collective-permute-start | bytes 786440 | tf_op jit(solution)/shard_map/ppermute | solution.py:300
  187.3 57.9 %collective-permute-start.38 = (f32[4,8,2048]{2,1,0:T(8,128)}, f32[4,8,2048]{2,1,0:T(8,128)S(1)}, u32[]{:S(2)}, u32[]{:S(2)}) collective-permute-start(f32[4,8,2048]{2,1,0:T(8,128)} %get-tuple-element.201), channel_id=1, source_target_pairs={{0,18},{2,16},{4,22},{6,20},{8,26},{10,24},{12,30},{14,28},{16,2},... | collective-permute-start | bytes 786440 | tf_op jit(solution)/shard_map/ppermute | solution.py:300
  193.5 57.8 %collective-permute-start.32 = (f32[4,8,2048]{2,1,0:T(8,128)}, f32[4,8,2048]{2,1,0:T(8,128)S(1)}, u32[]{:S(2)}, u32[]{:S(2)}) collective-permute-start(f32[4,8,2048]{2,1,0:T(8,128)} %get-tuple-element.188), channel_id=1, source_target_pairs={{0,22},{2,20},{4,18},{6,16},{8,30},{10,28},{12,26},{14,24},{16,6},... | collective-permute-start | bytes 786440 | tf_op jit(solution)/shard_map/ppermute | solution.py:300
  206.1 55.8 %collective-permute-start.43 = (f32[4,8,2048]{2,1,0:T(8,128)}, f32[4,8,2048]{2,1,0:T(8,128)S(1)}, u32[]{:S(2)}, u32[]{:S(2)}) collective-permute-start(f32[4,8,2048]{2,1,0:T(8,128)} %get-tuple-element.210), channel_id=1, source_target_pairs={{0,20},{2,22},{4,16},{6,18},{8,28},{10,30},{12,24},{14,26},{16,4},... | collective-permute-start | bytes 786440 | tf_op jit(solution)/shard_map/ppermute | solution.py:300
  206.1 61.2 %collective-permute-start.41 = (f32[4,8,2048]{2,1,0:T(8,128)}, f32[4,8,2048]{2,1,0:T(8,128)S(1)}, u32[]{:S(2)}, u32[]{:S(2)}) collective-permute-start(f32[4,8,2048]{2,1,0:T(8,128)} %get-tuple-element.206), channel_id=1, source_target_pairs={{0,16},{2,18},{4,20},{6,22},{8,24},{10,26},{12,28},{14,30},{16,0},... | collective-permute-start | bytes 786440 | tf_op jit(solution)/shard_map/ppermute | solution.py:300
  217.0 50.3 %collective-permute-start.42 = (f32[4,8,2048]{2,1,0:T(8,128)}, f32[4,8,2048]{2,1,0:T(8,128)S(1)}, u32[]{:S(2)}, u32[]{:S(2)}) collective-permute-start(f32[4,8,2048]{2,1,0:T(8,128)} %get-tuple-element.208), channel_id=1, source_target_pairs={{0,2},{2,0},{4,6},{6,4},{8,10},{10,8},{12,14},{14,12},{16,18},{18,... | collective-permute-start | bytes 786440 | tf_op jit(solution)/shard_map/ppermute | solution.py:300
  251.3 32.8 %collective-permute-start.46 = (f32[4,8,2048]{2,1,0:T(8,128)}, f32[4,8,2048]{2,1,0:T(8,128)S(1)}, u32[]{:S(2)}, u32[]{:S(2)}) collective-permute-start(f32[4,8,2048]{2,1,0:T(8,128)} %get-tuple-element.216), channel_id=1, source_target_pairs={{0,24},{2,26},{4,28},{6,30},{8,16},{10,18},{12,20},{14,22},{16,8},... | collective-permute-start | bytes 786440 | tf_op jit(solution)/shard_map/ppermute | solution.py:300
  303.6 40.6 %collective-permute-start.61 = (f32[4,8,2048]{2,1,0:T(8,128)}, f32[4,8,2048]{2,1,0:T(8,128)S(1)}, u32[]{:S(2)}, u32[]{:S(2)}) collective-permute-start(f32[4,8,2048]{2,1,0:T(8,128)} %get-tuple-element.245), channel_id=1, source_target_pairs={{0,22},{2,20},{4,18},{6,16},{8,30},{10,28},{12,26},{14,24},{16,6},... | collective-permute-start | bytes 786440 | tf_op jit(solution)/shard_map/ppermute | solution.py:300
  315.8 39.6 %collective-permute-start.36 = (f32[4,8,2048]{2,1,0:T(8,128)}, f32[4,8,2048]{2,1,0:T(8,128)S(1)}, u32[]{:S(2)}, u32[]{:S(2)}) collective-permute-start(f32[4,8,2048]{2,1,0:T(8,128)} %get-tuple-element.195), channel_id=1, source_target_pairs={{0,2},{2,0},{4,6},{6,4},{8,10},{10,8},{12,14},{14,12},{16,18},{18,... | collective-permute-start | bytes 786440 | tf_op jit(solution)/shard_map/ppermute | solution.py:300
  318.9 41.0 %collective-permute-start.33 = (f32[4,8,2048]{2,1,0:T(8,128)}, f32[4,8,2048]{2,1,0:T(8,128)S(1)}, u32[]{:S(2)}, u32[]{:S(2)}) collective-permute-start(f32[4,8,2048]{2,1,0:T(8,128)} %get-tuple-element.189), channel_id=1, source_target_pairs={{0,18},{2,16},{4,22},{6,20},{8,26},{10,24},{12,30},{14,28},{16,2},... | collective-permute-start | bytes 786440 | tf_op jit(solution)/shard_map/ppermute | solution.py:300
  346.4 31.0 %collective-permute-start.57 = (f32[4,8,2048]{2,1,0:T(8,128)}, f32[4,8,2048]{2,1,0:T(8,128)}, u32[]{:S(2)}, u32[]{:S(2)}) collective-permute-start(f32[4,8,2048]{2,1,0:T(8,128)} %get-tuple-element.237), channel_id=1, source_target_pairs={{0,12},{2,14},{4,8},{6,10},{8,4},{10,6},{12,0},{14,2},{16,28},{18,... | collective-permute-start | bytes 786440 | tf_op jit(solution)/shard_map/ppermute | solution.py:300
  377.4 33.6 %collective-permute-start.37 = (f32[4,8,2048]{2,1,0:T(8,128)}, f32[4,8,2048]{2,1,0:T(8,128)S(1)}, u32[]{:S(2)}, u32[]{:S(2)}) collective-permute-start(f32[4,8,2048]{2,1,0:T(8,128)} %get-tuple-element.196), channel_id=1, source_target_pairs={{0,14},{2,12},{4,10},{6,8},{8,6},{10,4},{12,2},{14,0},{16,30},{18,... | collective-permute-start | bytes 786440 | tf_op jit(solution)/shard_map/ppermute | solution.py:300
  377.4 33.6 %collective-permute-start.53 = (f32[4,8,2048]{2,1,0:T(8,128)}, f32[4,8,2048]{2,1,0:T(8,128)S(1)}, u32[]{:S(2)}, u32[]{:S(2)}) collective-permute-start(f32[4,8,2048]{2,1,0:T(8,128)} %get-tuple-element.229), channel_id=1, source_target_pairs={{0,28},{2,30},{4,24},{6,26},{8,20},{10,22},{12,16},{14,18},{16,12}... | collective-permute-start | bytes 786440 | tf_op jit(solution)/shard_map/ppermute | solution.py:300
  381.4 32.5 %collective-permute-start.34 = (f32[4,8,2048]{2,1,0:T(8,128)}, f32[4,8,2048]{2,1,0:T(8,128)S(1)}, u32[]{:S(2)}, u32[]{:S(2)}) collective-permute-start(f32[4,8,2048]{2,1,0:T(8,128)} %get-tuple-element.190), channel_id=1, source_target_pairs={{0,30},{2,28},{4,26},{6,24},{8,22},{10,20},{12,18},{14,16},{16,14}... | collective-permute-start | bytes 786440 | tf_op jit(solution)/shard_map/ppermute | solution.py:300
  (88 other events, 3558.4 us)

commit v3 on v2

--- a/solution.py
+++ b/solution.py
@@ -11,7 +11,7 @@
 ITERS = 3
 CHUNKS = 2
 FAR = 6
-NEAR = 6
+NEAR = 7
 LATER = 1
 HEAD = (1, 3, 4)
 TAIL = 3
@@ -258,13 +258,14 @@
             due.append((half * (CHUNKS + c + 1) + FAR, ("weights", c, tuple([0] + flips))))
     due.sort(key=lambda one: one[0])
     steps, gone = [], 0
+    lasts = [flip for flip in far if flip != far[half // 2]] + [far[half // 2]]
     first = woven(far[half // 2:half // 2 + LEAD] + far[:half // 2] + far[half // 2 + LEAD:], near)
     heads = cut(first + [0], HEAD)
     steps.append(("momentum", 0, heads[0]))
     rest, ready = heads[1:], set(heads[0])
     for kind in ("in", "out"):
         for c in range(CHUNKS):
-            order = flips if (kind, c) != ("out", CHUNKS - 1) else woven(far[:-TAIL], near) + far[-TAIL:]
+            order = flips if (kind, c) != ("out", CHUNKS - 1) else woven(lasts[:-TAIL], near) + lasts[-TAIL:]
             order = first if (kind, c) == ("in", 0) else order
             for flip in order:
                 while kind == "in" and c == 0 and flip not in ready:

time: 417 us -> 412 us (0.988)
  the two profiles are of different devices: /device:TPU:1 before, /device:TPU:12 now
where the time goes in v3:
time: 412 us; the launch traced here: 410 us
  waiting for transfers between devices  230 us (56%)
  Pallas kernels  95.4 us (23%)
  starting transfers between devices  82.2 us (20%)
    ppermute x60, waiting for transfers between devices, send(): lax.ppermute(piece, 'shard', [(i, i ^ flip) for i in range(owners)])  230 us
    ppermute x60, starting transfers between devices, send(): lax.ppermute(piece, 'shard', [(i, i ^ flip) for i in range(owners)])  79.1 us
    pallas_call x5, Pallas kernels, momentum_of(): pl.pallas_call(functools.partial(momentum_kernel, count), grid_spec=pltpu...  29.4 us
    pallas_call x2, Pallas kernels, apply_of(): pl.pallas_call(functools.partial(apply_kernel, len(grams), len(pieces)),...  27.9 us
    pallas_call x4, Pallas kernels, weights_of(): pl.pallas_call(functools.partial(weights_kernel, count), grid_spec=pltpu....  23.8 us
    pallas_call x2, Pallas kernels, gram_of(): pl.pallas_call(gram_kernel, grid=(held,), in_specs=[pl.BlockSpec((1, rows...  12.5 us
  transfers between devices with their start and end apart: 62, of which 33 were waited for; matrix products, arithmetic and copies ran while one was open for 0% of the time, Pallas kernels for 23%

profile of v3, /device:TPU:12, one launch (start us, length us, event | category | flops | bytes accessed | tf_op | source)
XLA Modules:
  0.0 410.1 jit_solution(6290396860989519416)
XLA Ops:
  14.4 14.1 %collective-permute-done.22.refs_12_.refs_14_ = f32[4,8,2048]{2,1,0:T(8,128)S(1)} collective-permute-done((f32[4,8,2048]{2,1,0:T(8,128)}, f32[4,8,2048]{2,1,0:T(8,128)S(1)}, u32[]{:S(2)}, u32[]{:S(2)}) %collective-permute-start.22) | collective-permute-done | bytes 262176 | tf_op jit(solution)/shard_map/ppermute | solution.py:301
  28.6 7.1 %momentum.8 = (f32[128,8,2048]{2,1,0:T(8,128)}, f32[4,8,2048]{2,1,0:T(8,128)}, f32[4,8,2048]{2,1,0:T(8,128)}, f32[4,8,2048]{2,1,0:T(8,128)}, f32[4,8,2048]{2,1,0...) custom-call(s32[1]{0:T(128)} %bitcast.me_ref, ...), custom_call_target="tpu_custom_call", output_to_operand_aliasing={{0}: (3, {})} | custom-call | flops 1048576 | bytes 8388608 | tf_op jit(solution)/shard_map/momentum/pallas_call | solution.py:90
  35.6 13.1 %momentum.9 = (f32[128,8,2048]{2,1,0:T(8,128)}, f32[4,8,2048]{2,1,0:T(8,128)}, f32[4,8,2048]{2,1,0:T(8,128)}, f32[4,8,2048]{2,1,0:T(8,128)}, f32[4,8,2048]{2,1,0...) custom-call(s32[1]{0:T(128)} %bitcast.me_ref, ...), custom_call_target="tpu_custom_call", output_to_operand_aliasing={{0}: (3, {})} | custom-call | flops 2097152 | bytes 16777216 | tf_op jit(solution)/shard_map/momentum/pallas_call | solution.py:90
  60.2 9.6 %collective-permute-start.8 = (f32[4,8,2048]{2,1,0:T(8,128)S(1)}, f32[4,8,2048]{2,1,0:T(8,128)S(1)}, u32[]{:S(2)}, u32[]{:S(2)}) collective-permute-start(f32[4,8,2048]{2,1,0:T(8,128)S(1)} %copy-done.46), channel_id=1, source_target_pairs={{0,10},{2,8},{4,14},{6,12},{8,2},{10,0},{12,6},{14,4},{16,26},{18,... | collective-permute-start | bytes 786440 | tf_op jit(solution)/shard_map/ppermute | solution.py:301
  74.7 5.6 %collective-permute-done.18.refs_11_.refs_13_ = f32[4,8,2048]{2,1,0:T(8,128)S(1)} collective-permute-done((f32[4,8,2048]{2,1,0:T(8,128)}, f32[4,8,2048]{2,1,0:T(8,128)S(1)}, u32[]{:S(2)}, u32[]{:S(2)}) %collective-permute-start.18) | collective-permute-done | bytes 262176 | tf_op jit(solution)/shard_map/ppermute | solution.py:301
  88.0 29.8 %collective-permute-done.26.refs_15_.refs_17_ = f32[4,8,2048]{2,1,0:T(8,128)S(1)} collective-permute-done((f32[4,8,2048]{2,1,0:T(8,128)S(1)}, f32[4,8,2048]{2,1,0:T(8,128)S(1)}, u32[]{:S(2)}, u32[]{:S(2)}) %collective-permute-start.26) | collective-permute-done | bytes 262176 | tf_op jit(solution)/shard_map/ppermute | solution.py:301
  117.8 10.4 %collective-permute-done.23.refs_14_.refs_16_ = f32[4,8,2048]{2,1,0:T(8,128)S(1)} collective-permute-done((f32[4,8,2048]{2,1,0:T(8,128)S(1)}, f32[4,8,2048]{2,1,0:T(8,128)S(1)}, u32[]{:S(2)}, u32[]{:S(2)}) %collective-permute-start.23) | collective-permute-done | bytes 262176 | tf_op jit(solution)/shard_map/ppermute | solution.py:301
  134.2 6.3 %gram.2.refs_0_ = f32[4,128,128]{2,1,0:T(8,128)} custom-call(f32[4,8,2048]{2,1,0:T(8,128)} %get-tuple-element.178.refs_0_.refs_2_, f32[4,8,2048]{2,1,0:T(8,128)} %copy-done.19, f32[4,8,2048]{2,1,0:T(8,128)} %copy-done.20, f32[4,8,2048]{2,1,0:T(8,128)} %copy-done.27, f32[4,8,2048]{2,1,0:T(8,128)} %copy-done.32, f32[4,8,2048]{2,1,0:T(8,128)} %copy-done.37, ...), custom_call_target="tpu_custom_call" | custom-call | flops 1610612736 | bytes 4194304 | tf_op jit(solution)/shard_map/gram/pallas_call | solution.py:194
  153.9 5.6 %collective-permute-done.11.refs_6_.refs_8_ = f32[4,8,2048]{2,1,0:T(8,128)S(1)} collective-permute-done((f32[4,8,2048]{2,1,0:T(8,128)}, f32[4,8,2048]{2,1,0:T(8,128)S(1)}, u32[]{:S(2)}, u32[]{:S(2)}) %collective-permute-start.11) | collective-permute-done | bytes 262176 | tf_op jit(solution)/shard_map/ppermute | solution.py:301
  159.5 7.1 %collective-permute-start.24 = (f32[4,8,2048]{2,1,0:T(8,128)}, f32[4,8,2048]{2,1,0:T(8,128)}, u32[]{:S(2)}, u32[]{:S(2)}) collective-permute-start(f32[4,8,2048]{2,1,0:T(8,128)} %get-tuple-element.171), channel_id=1, source_target_pairs={{0,24},{2,26},{4,28},{6,30},{8,16},{10,18},{12,20},{14,22},{16,8},... | collective-permute-start | bytes 786440 | tf_op jit(solution)/shard_map/ppermute | solution.py:301
  170.9 14.0 %apply.2 = (f32[4,8,2048]{2,1,0:T(8,128)}, f32[4,8,2048]{2,1,0:T(8,128)}, f32[4,8,2048]{2,1,0:T(8,128)}, f32[4,8,2048]{2,1,0:T(8,128)}, f32[4,8,2048]{2,1,0:T(8,...) custom-call(f32[4,128,128]{2,1,0:T(8,128)} %gram.2.refs_0_, ...), custom_call_target="tpu_custom_call" | custom-call | flops 2516582400 | bytes 8388608 | tf_op jit(solution)/shard_map/apply/pallas_call | solution.py:220
  194.2 6.0 %collective-permute-done.5.refs_3_.refs_5_ = f32[4,8,2048]{2,1,0:T(8,128)S(1)} collective-permute-done((f32[4,8,2048]{2,1,0:T(8,128)S(1)}, f32[4,8,2048]{2,1,0:T(8,128)S(1)}, u32[]{:S(2)}, u32[]{:S(2)}) %collective-permute-start.5) | collective-permute-done | bytes 262176 | tf_op jit(solution)/shard_map/ppermute | solution.py:301
  200.2 5.5 %collective-permute-done.3.refs_2_.refs_4_ = f32[4,8,2048]{2,1,0:T(8,128)S(1)} collective-permute-done((f32[4,8,2048]{2,1,0:T(8,128)S(1)}, f32[4,8,2048]{2,1,0:T(8,128)S(1)}, u32[]{:S(2)}, u32[]{:S(2)}) %collective-permute-start.3) | collective-permute-done | bytes 262176 | tf_op jit(solution)/shard_map/ppermute | solution.py:301
  209.7 22.2 %collective-permute-done.30.refs_15_.refs_17_ = f32[4,8,2048]{2,1,0:T(8,128)S(1)} collective-permute-done((f32[4,8,2048]{2,1,0:T(8,128)S(1)}, f32[4,8,2048]{2,1,0:T(8,128)S(1)}, u32[]{:S(2)}, u32[]{:S(2)}) %collective-permute-start.30) | collective-permute-done | bytes 262176 | tf_op jit(solution)/shard_map/ppermute | solution.py:301
  232.6 6.3 %gram.3.refs_0_ = f32[4,128,128]{2,1,0:T(8,128)} custom-call(f32[4,8,2048]{2,1,0:T(8,128)} %get-tuple-element.127.refs_0_.refs_2_, f32[4,8,2048]{2,1,0:T(8,128)} %copy-done.42, f32[4,8,2048]{2,1,0:T(8,128)} %copy-done.40, f32[4,8,2048]{2,1,0:T(8,128)} %copy-done.38, f32[4,8,2048]{2,1,0:T(8,128)} %copy-done.29, f32[4,8,2048]{2,1,0:T(8,128)} %copy-done.28, ...), custom_call_target="tpu_custom_call" | custom-call | flops 1610612736 | bytes 4194304 | tf_op jit(solution)/shard_map/gram/pallas_call | solution.py:194
  261.0 13.9 %apply.3 = (f32[4,8,2048]{2,1,0:T(8,128)}, f32[4,8,2048]{2,1,0:T(8,128)}, f32[4,8,2048]{2,1,0:T(8,128)}, f32[4,8,2048]{2,1,0:T(8,128)}, f32[4,8,2048]{2,1,0:T(8,...) custom-call(f32[4,128,128]{2,1,0:T(8,128)} %gram.3.refs_0_, ...), custom_call_target="tpu_custom_call" | custom-call | flops 2516582400 | bytes 8388608 | tf_op jit(solution)/shard_map/apply/pallas_call | solution.py:220
  278.8 5.7 %collective-permute-done.45.refs_8_ = f32[4,8,2048]{2,1,0:T(8,128)} collective-permute-done((f32[4,8,2048]{2,1,0:T(8,128)}, f32[4,8,2048]{2,1,0:T(8,128)}, u32[]{:S(2)}, u32[]{:S(2)}) %collective-permute-start.45) | collective-permute-done | bytes 262176 | tf_op jit(solution)/shard_map/ppermute | solution.py:301
  289.0 20.1 %collective-permute-done.50.refs_13_ = f32[4,8,2048]{2,1,0:T(8,128)S(1)} collective-permute-done((f32[4,8,2048]{2,1,0:T(8,128)}, f32[4,8,2048]{2,1,0:T(8,128)S(1)}, u32[]{:S(2)}, u32[]{:S(2)}) %collective-permute-start.50) | collective-permute-done | bytes 262176 | tf_op jit(solution)/shard_map/ppermute | solution.py:301
  309.2 10.2 %collective-permute-done.38.refs_15_ = f32[4,8,2048]{2,1,0:T(8,128)S(1)} collective-permute-done((f32[4,8,2048]{2,1,0:T(8,128)}, f32[4,8,2048]{2,1,0:T(8,128)S(1)}, u32[]{:S(2)}, u32[]{:S(2)}) %collective-permute-start.38) | collective-permute-done | bytes 262176 | tf_op jit(solution)/shard_map/ppermute | solution.py:301
  319.4 11.2 %collective-permute-done.61.refs_7_ = f32[4,8,2048]{2,1,0:T(8,128)S(1)} collective-permute-done((f32[4,8,2048]{2,1,0:T(8,128)}, f32[4,8,2048]{2,1,0:T(8,128)S(1)}, u32[]{:S(2)}, u32[]{:S(2)}) %collective-permute-start.61) | collective-permute-done | bytes 262176 | tf_op jit(solution)/shard_map/ppermute | solution.py:301
  341.9 11.2 %collective-permute-done.33.refs_3_ = f32[4,8,2048]{2,1,0:T(8,128)S(1)} collective-permute-done((f32[4,8,2048]{2,1,0:T(8,128)}, f32[4,8,2048]{2,1,0:T(8,128)S(1)}, u32[]{:S(2)}, u32[]{:S(2)}) %collective-permute-start.33) | collective-permute-done | bytes 262176 | tf_op jit(solution)/shard_map/ppermute | solution.py:301
  353.2 11.3 %weights.4.refs_8_ = f32[128,8,2048]{2,1,0:T(8,128)} custom-call(s32[1]{0:T(128)} %bitcast.2.me_ref, f32[128,8,2048]{2,1,0:T(8,128)} %weights_ref.9, f32[4,8,2048]{2,1,0:T(8,128)S(1)} %copy-done, f32[4,8,2048]{2,1,0:T(8,128)S(1)} %collective-permute-done.40.refs_1_, f32[4,8,2048]{2,1,0:T(8,128)S(1)} %collective-permute-done.41.refs_2_, ...), custom_call_target="tpu_custom_call" | custom-call | flops 3145728 | bytes 12582912 | tf_op jit(solution)/shard_map/weights/pallas_call | solution.py:120
  371.7 6.0 %weights.5.refs_4_ = f32[128,8,2048]{2,1,0:T(8,128)} custom-call(s32[1]{0:T(128)} %bitcast.1.me_ref, f32[128,8,2048]{2,1,0:T(8,128)} %weights_ref.9, f32[4,8,2048]{2,1,0:T(8,128)S(1)} %copy-done.1, f32[4,8,2048]{2,1,0:T(8,128)S(1)} %collective-permute-done.51.refs_1_, ...), custom_call_target="tpu_custom_call", output_to_operand_aliasing={{}: (10, {})} | custom-call | flops 1572864 | bytes 6291456 | tf_op jit(solution)/shard_map/weights/pallas_call | solution.py:120
  383.7 19.2 %collective-permute-done.52.refs_2_ = f32[4,8,2048]{2,1,0:T(8,128)S(1)} collective-permute-done((f32[4,8,2048]{2,1,0:T(8,128)}, f32[4,8,2048]{2,1,0:T(8,128)S(1)}, u32[]{:S(2)}, u32[]{:S(2)}) %collective-permute-start.52) | collective-permute-done | bytes 262176 | tf_op jit(solution)/shard_map/ppermute | solution.py:301
  (211 shorter events, 137.4 us)
Async XLA Ops:
  7.4 41.4 %collective-permute-start = (f32[4,8,2048]{2,1,0:T(8,128)}, f32[4,8,2048]{2,1,0:T(8,128)S(1)}, u32[]{:S(2)}, u32[]{:S(2)}) collective-permute-start(f32[4,8,2048]{2,1,0:T(8,128)} %get-tuple-element.130), channel_id=1, source_target_pairs={{0,2},{2,0},{4,6},{6,4},{8,10},{10,8},{12,14},{14,12},{16,18},{18,... | collective-permute-start | bytes 786440 | tf_op jit(solution)/shard_map/ppermute | solution.py:301
  7.4 43.4 %collective-permute-start.2 = (f32[4,8,2048]{2,1,0:T(8,128)}, f32[4,8,2048]{2,1,0:T(8,128)S(1)}, u32[]{:S(2)}, u32[]{:S(2)}) collective-permute-start(f32[4,8,2048]{2,1,0:T(8,128)} %get-tuple-element.133), channel_id=1, source_target_pairs={{0,4},{2,6},{4,0},{6,2},{8,12},{10,14},{12,8},{14,10},{16,20},{18,... | collective-permute-start | bytes 786440 | tf_op jit(solution)/shard_map/ppermute | solution.py:301
  8.0 42.8 %collective-permute-start.25 = (f32[4,8,2048]{2,1,0:T(8,128)}, f32[4,8,2048]{2,1,0:T(8,128)S(1)}, u32[]{:S(2)}, u32[]{:S(2)}) collective-permute-start(f32[4,8,2048]{2,1,0:T(8,128)} %get-tuple-element.174), channel_id=1, source_target_pairs={{0,16},{2,18},{4,20},{6,22},{8,24},{10,26},{12,28},{14,30},{16,0},... | collective-permute-start | bytes 786440 | tf_op jit(solution)/shard_map/ppermute | solution.py:301
  13.0 40.5 %collective-permute-start.14 = (f32[4,8,2048]{2,1,0:T(8,128)}, f32[4,8,2048]{2,1,0:T(8,128)S(1)}, u32[]{:S(2)}, u32[]{:S(2)}) collective-permute-start(f32[4,8,2048]{2,1,0:T(8,128)} %get-tuple-element.152), channel_id=1, source_target_pairs={{0,18},{2,16},{4,22},{6,20},{8,26},{10,24},{12,30},{14,28},{16,2},... | collective-permute-start | bytes 786440 | tf_op jit(solution)/shard_map/ppermute | solution.py:301
  74.7 43.1 %collective-permute-start.26 = (f32[4,8,2048]{2,1,0:T(8,128)S(1)}, f32[4,8,2048]{2,1,0:T(8,128)S(1)}, u32[]{:S(2)}, u32[]{:S(2)}) collective-permute-start(f32[4,8,2048]{2,1,0:T(8,128)S(1)} %copy-done.45), channel_id=1, source_target_pairs={{0,30},{2,28},{4,26},{6,24},{8,22},{10,20},{12,18},{14,16},{16,14}... | collective-permute-start | bytes 786440 | tf_op jit(solution)/shard_map/ppermute | solution.py:301
  80.3 47.8 %collective-permute-start.23 = (f32[4,8,2048]{2,1,0:T(8,128)S(1)}, f32[4,8,2048]{2,1,0:T(8,128)S(1)}, u32[]{:S(2)}, u32[]{:S(2)}) collective-permute-start(f32[4,8,2048]{2,1,0:T(8,128)S(1)} %copy-done.43), channel_id=1, source_target_pairs={{0,28},{2,30},{4,24},{6,26},{8,20},{10,22},{12,16},{14,18},{16,12}... | collective-permute-start | bytes 786440 | tf_op jit(solution)/shard_map/ppermute | solution.py:301
  81.6 50.6 %collective-permute-start.21 = (f32[4,8,2048]{2,1,0:T(8,128)}, f32[4,8,2048]{2,1,0:T(8,128)S(1)}, u32[]{:S(2)}, u32[]{:S(2)}) collective-permute-start(f32[4,8,2048]{2,1,0:T(8,128)} %get-tuple-element.165), channel_id=1, source_target_pairs={{0,22},{2,20},{4,18},{6,16},{8,30},{10,28},{12,26},{14,24},{16,6},... | collective-permute-start | bytes 786440 | tf_op jit(solution)/shard_map/ppermute | solution.py:301
  85.8 54.7 %collective-permute-start.19 = (f32[4,8,2048]{2,1,0:T(8,128)}, f32[4,8,2048]{2,1,0:T(8,128)S(1)}, u32[]{:S(2)}, u32[]{:S(2)}) collective-permute-start(f32[4,8,2048]{2,1,0:T(8,128)} %get-tuple-element.160), channel_id=1, source_target_pairs={{0,20},{2,22},{4,16},{6,18},{8,28},{10,30},{12,24},{14,26},{16,4},... | collective-permute-start | bytes 786440 | tf_op jit(solution)/shard_map/ppermute | solution.py:301
  86.4 57.0 %collective-permute-start.17 = (f32[4,8,2048]{2,1,0:T(8,128)}, f32[4,8,2048]{2,1,0:T(8,128)S(1)}, u32[]{:S(2)}, u32[]{:S(2)}) collective-permute-start(f32[4,8,2048]{2,1,0:T(8,128)} %get-tuple-element.156), channel_id=1, source_target_pairs={{0,18},{2,16},{4,22},{6,20},{8,26},{10,24},{12,30},{14,28},{16,2},... | collective-permute-start | bytes 786440 | tf_op jit(solution)/shard_map/ppermute | solution.py:301
  143.4 41.6 %collective-permute-start.9 = (f32[4,8,2048]{2,1,0:T(8,128)}, f32[4,8,2048]{2,1,0:T(8,128)S(1)}, u32[]{:S(2)}, u32[]{:S(2)}) collective-permute-start(f32[4,8,2048]{2,1,0:T(8,128)} %get-tuple-element.143), channel_id=1, source_target_pairs={{0,10},{2,8},{4,14},{6,12},{8,2},{10,0},{12,6},{14,4},{16,26},{18,... | collective-permute-start | bytes 786440 | tf_op jit(solution)/shard_map/ppermute | solution.py:301
  148.3 38.6 %collective-permute-start.7 = (f32[4,8,2048]{2,1,0:T(8,128)}, f32[4,8,2048]{2,1,0:T(8,128)S(1)}, u32[]{:S(2)}, u32[]{:S(2)}) collective-permute-start(f32[4,8,2048]{2,1,0:T(8,128)} %get-tuple-element.140), channel_id=1, source_target_pairs={{0,8},{2,10},{4,12},{6,14},{8,0},{10,2},{12,4},{14,6},{16,24},{18,... | collective-permute-start | bytes 786440 | tf_op jit(solution)/shard_map/ppermute | solution.py:301
  153.9 35.1 %collective-permute-start.27 = (f32[4,8,2048]{2,1,0:T(8,128)}, f32[4,8,2048]{2,1,0:T(8,128)S(1)}, u32[]{:S(2)}, u32[]{:S(2)}) collective-permute-start(f32[4,8,2048]{2,1,0:T(8,128)} %get-tuple-element.176), channel_id=1, source_target_pairs={{0,26},{2,24},{4,30},{6,28},{8,18},{10,16},{12,22},{14,20},{16,10}... | collective-permute-start | bytes 786440 | tf_op jit(solution)/shard_map/ppermute | solution.py:301
  189.1 42.7 %collective-permute-start.30 = (f32[4,8,2048]{2,1,0:T(8,128)S(1)}, f32[4,8,2048]{2,1,0:T(8,128)S(1)}, u32[]{:S(2)}, u32[]{:S(2)}) collective-permute-start(f32[4,8,2048]{2,1,0:T(8,128)S(1)} %copy-done.11), channel_id=1, source_target_pairs={{0,30},{2,28},{4,26},{6,24},{8,22},{10,20},{12,18},{14,16},{16,14}... | collective-permute-start | bytes 786440 | tf_op jit(solution)/shard_map/ppermute | solution.py:301
  192.0 46.9 %collective-permute-start.37 = (f32[4,8,2048]{2,1,0:T(8,128)}, f32[4,8,2048]{2,1,0:T(8,128)S(1)}, u32[]{:S(2)}, u32[]{:S(2)}) collective-permute-start(f32[4,8,2048]{2,1,0:T(8,128)} %get-tuple-element.197), channel_id=1, source_target_pairs={{0,18},{2,16},{4,22},{6,20},{8,26},{10,24},{12,30},{14,28},{16,2},... | collective-permute-start | bytes 786440 | tf_op jit(solution)/shard_map/ppermute | solution.py:301
  200.2 40.9 %collective-permute-start.32 = (f32[4,8,2048]{2,1,0:T(8,128)}, f32[4,8,2048]{2,1,0:T(8,128)S(1)}, u32[]{:S(2)}, u32[]{:S(2)}) collective-permute-start(f32[4,8,2048]{2,1,0:T(8,128)} %get-tuple-element.186), channel_id=1, source_target_pairs={{0,22},{2,20},{4,18},{6,16},{8,30},{10,28},{12,26},{14,24},{16,6},... | collective-permute-start | bytes 786440 | tf_op jit(solution)/shard_map/ppermute | solution.py:301
  205.7 41.0 %collective-permute-start.43 = (f32[4,8,2048]{2,1,0:T(8,128)}, f32[4,8,2048]{2,1,0:T(8,128)S(1)}, u32[]{:S(2)}, u32[]{:S(2)}) collective-permute-start(f32[4,8,2048]{2,1,0:T(8,128)} %get-tuple-element.208), channel_id=1, source_target_pairs={{0,20},{2,22},{4,16},{6,18},{8,28},{10,30},{12,24},{14,26},{16,4},... | collective-permute-start | bytes 786440 | tf_op jit(solution)/shard_map/ppermute | solution.py:301
  206.6 45.7 %collective-permute-start.40 = (f32[4,8,2048]{2,1,0:T(8,128)}, f32[4,8,2048]{2,1,0:T(8,128)S(1)}, u32[]{:S(2)}, u32[]{:S(2)}) collective-permute-start(f32[4,8,2048]{2,1,0:T(8,128)} %get-tuple-element.202), channel_id=1, source_target_pairs={{0,16},{2,18},{4,20},{6,22},{8,24},{10,26},{12,28},{14,30},{16,0},... | collective-permute-start | bytes 786440 | tf_op jit(solution)/shard_map/ppermute | solution.py:301
  278.6 40.8 %collective-permute-start.38 = (f32[4,8,2048]{2,1,0:T(8,128)}, f32[4,8,2048]{2,1,0:T(8,128)S(1)}, u32[]{:S(2)}, u32[]{:S(2)}) collective-permute-start(f32[4,8,2048]{2,1,0:T(8,128)} %get-tuple-element.198), channel_id=1, source_target_pairs={{0,30},{2,28},{4,26},{6,24},{8,22},{10,20},{12,18},{14,16},{16,14}... | collective-permute-start | bytes 786440 | tf_op jit(solution)/shard_map/ppermute | solution.py:301
  284.5 46.1 %collective-permute-start.61 = (f32[4,8,2048]{2,1,0:T(8,128)}, f32[4,8,2048]{2,1,0:T(8,128)S(1)}, u32[]{:S(2)}, u32[]{:S(2)}) collective-permute-start(f32[4,8,2048]{2,1,0:T(8,128)} %get-tuple-element.243), channel_id=1, source_target_pairs={{0,22},{2,20},{4,18},{6,16},{8,30},{10,28},{12,26},{14,24},{16,6},... | collective-permute-start | bytes 786440 | tf_op jit(solution)/shard_map/ppermute | solution.py:301
  288.8 42.0 %collective-permute-start.60 = (f32[4,8,2048]{2,1,0:T(8,128)}, f32[4,8,2048]{2,1,0:T(8,128)S(1)}, u32[]{:S(2)}, u32[]{:S(2)}) collective-permute-start(f32[4,8,2048]{2,1,0:T(8,128)} %get-tuple-element.241), channel_id=1, source_target_pairs={{0,6},{2,4},{4,2},{6,0},{8,14},{10,12},{12,10},{14,8},{16,22},{18,... | collective-permute-start | bytes 786440 | tf_op jit(solution)/shard_map/ppermute | solution.py:301
  288.8 47.5 %collective-permute-start.59 = (f32[4,8,2048]{2,1,0:T(8,128)}, f32[4,8,2048]{2,1,0:T(8,128)S(1)}, u32[]{:S(2)}, u32[]{:S(2)}) collective-permute-start(f32[4,8,2048]{2,1,0:T(8,128)} %get-tuple-element.239), channel_id=1, source_target_pairs={{0,20},{2,22},{4,16},{6,18},{8,28},{10,30},{12,24},{14,26},{16,4},... | collective-permute-start | bytes 786440 | tf_op jit(solution)/shard_map/ppermute | solution.py:301
  330.6 33.9 %collective-permute-start.58 = (f32[4,8,2048]{2,1,0:T(8,128)}, f32[4,8,2048]{2,1,0:T(8,128)S(1)}, u32[]{:S(2)}, u32[]{:S(2)}) collective-permute-start(f32[4,8,2048]{2,1,0:T(8,128)} %get-tuple-element.237), channel_id=1, source_target_pairs={{0,4},{2,6},{4,0},{6,2},{8,12},{10,14},{12,8},{14,10},{16,20},{18,... | collective-permute-start | bytes 786440 | tf_op jit(solution)/shard_map/ppermute | solution.py:301
  330.8 36.5 %collective-permute-start.56 = (f32[4,8,2048]{2,1,0:T(8,128)}, f32[4,8,2048]{2,1,0:T(8,128)S(1)}, u32[]{:S(2)}, u32[]{:S(2)}) collective-permute-start(f32[4,8,2048]{2,1,0:T(8,128)} %get-tuple-element.233), channel_id=1, source_target_pairs={{0,12},{2,14},{4,8},{6,10},{8,4},{10,6},{12,0},{14,2},{16,28},{18,... | collective-permute-start | bytes 786440 | tf_op jit(solution)/shard_map/ppermute | solution.py:301
  369.5 39.8 %collective-permute-start.34 = (f32[4,8,2048]{2,1,0:T(8,128)}, f32[4,8,2048]{2,1,0:T(8,128)S(1)}, u32[]{:S(2)}, u32[]{:S(2)}) collective-permute-start(f32[4,8,2048]{2,1,0:T(8,128)} %get-tuple-element.188), channel_id=1, source_target_pairs={{0,24},{2,26},{4,28},{6,30},{8,16},{10,18},{12,20},{14,22},{16,8},... | collective-permute-start | bytes 786440 | tf_op jit(solution)/shard_map/ppermute | solution.py:301
  (86 other events, 3312.7 us)
